TPU v7x, 128 devices: a whole 4x4x4 slice. The times are simulated.
128 devices in a mesh: gx: 8 (over z, core), yz: 16 (over y, x).
Axes of the slice: x: 4, y: 4, z: 4, core: 2. Of those that a mesh axis runs over, the one named last changes fastest.
Arguments:
- brick_ids: int32 [16384, 1], P(('gx', 'yz')), may hold values from 0 to 127; in each aligned block of 128 rows (0 to 127, 128 to 255, ...) at most 2 rows name the same one
- voxel_offset: int32 [16384, 256], P(('gx', 'yz')), may hold values from 0 to 4095
- fractions: float32 [16384, 3, 256], P(('gx', 'yz')), may hold values from 0 to 1
- normals: float32 [16384, 3, 256], P(('gx', 'yz')), may hold values from -6 to 6
- point_weight: float32 [16384, 256], P(('gx', 'yz')), may hold values from 0.1 to 10
- tile_count: int32 [128], P(('gx', 'yz')), may hold values from 96 to 128, as said below
Outputs:
- rhs: float32 [32, 128, 128], P('gx', 'yz')
- screen: float32 [32, 128, 128], P('gx', 'yz')
Inputs may be any that keep to these rules, and one draw needn't show every extreme that they name: `brick_ids`: brick b belongs to index b // 16 of gx and b % 16 of yz. Among the 128 tile slots of one device no brick is named more than 2 times. `tile_count`: some device has all its slots valid in every draw.
All inputs are finite; a program needn't handle non-finite values.
Results may differ from a plain program's by a relative error of at most 0.0039.
Values sent between devices are 32-bit elements; how exact they have to be, the bound alone decides.
No kernel may reach another device: no remote copies, remote signals or barrier semaphores. Data moves between devices by JAX's collectives and lax.ppermute only.
A program may use at most 64 MiB of HBM per device.

v0:
```python
import jax
import jax.numpy as jnp
from jax import lax
from jax.sharding import PartitionSpec as P

BX = 4
BY = 8
BZ = 128


def passed_along(value, axis, steps):
    count = lax.axis_size(axis)
    first, last = (max(0, -steps), min(count, count - steps))
    return lax.ppermute(value, axis, [(source, source + steps) for source in range(first, last)])


def spline(frac):
    weights = [0.5 * (1.0 - frac) ** 2, 0.75 - (frac - 0.5) ** 2, 0.5 * frac * frac]
    slopes = [frac - 1.0, 1.0 - 2.0 * frac, frac]
    return (weights, slopes)


def splat_block(carry, points):
    rhs_acc, screen_acc = carry
    channels = jnp.transpose(points, (1, 0, 2)).reshape(8, -1)
    offset = channels[0].astype(jnp.int32)
    cell_x = offset // (BY * BZ)
    cell_y = offset // BZ % BY
    cell_z = offset % BZ
    wx, gx = spline(channels[1])
    wy, gy = spline(channels[2])
    wz, gz = spline(channels[3])
    nx = channels[4]
    ny = channels[5]
    nz = channels[6]
    weight = channels[7]
    plane_rows = jnp.arange((BX + 2) * (BY + 2), dtype=jnp.int32)[:, None]
    depth_cols = jnp.arange(BZ, dtype=jnp.int32)[None, :]
    count = offset.shape[0]
    a_twelve = jnp.zeros(((BX + 2) * (BY + 2), count), jnp.float32)
    a_three = jnp.zeros_like(a_twelve)
    a_screen = jnp.zeros_like(a_twelve)
    for first in range(3):
        for second in range(3):
            target = ((cell_x + first) * (BY + 2) + cell_y + second)[None, :]
            hit = plane_rows == target
            term_twelve = nx * gx[first] * wy[second] + ny * wx[first] * gy[second]
            term_three = nz * wx[first] * wy[second]
            term_screen = weight * wx[first] * wy[second]
            a_twelve = a_twelve + jnp.where(hit, term_twelve[None, :], 0.0)
            a_three = a_three + jnp.where(hit, term_three[None, :], 0.0)
            a_screen = a_screen + jnp.where(hit, term_screen[None, :], 0.0)
    z_value = jnp.zeros((count, BZ), jnp.float32)
    z_slope = jnp.zeros_like(z_value)
    for third in range(3):
        hit = (cell_z + third - 1)[:, None] == depth_cols
        z_value = z_value + jnp.where(hit, wz[third][:, None], 0.0)
        z_slope = z_slope + jnp.where(hit, gz[third][:, None], 0.0)
    z_value = z_value.astype(jnp.bfloat16)
    left = jnp.concatenate([a_twelve, a_three], axis=1).astype(jnp.bfloat16)
    right = jnp.concatenate([z_value, z_slope.astype(jnp.bfloat16)], axis=0)
    rhs_acc = rhs_acc + jnp.dot(left, right, preferred_element_type=jnp.float32)
    screen_acc = screen_acc + jnp.dot(
        a_screen.astype(jnp.bfloat16), z_value, preferred_element_type=jnp.float32
    )
    return ((rhs_acc, screen_acc), None)


def shards(brick_ids, voxel_offset, fractions, normals, point_weight, tile_count):
    n_slabs = lax.axis_size("gx")
    n_columns = lax.axis_size("yz")
    devices = n_slabs * n_columns
    tiles_here = brick_ids.shape[0]
    tile_len = voxel_offset.shape[1]
    capacity = max(2, (tiles_here + devices - 1) // devices)
    dest = brick_ids[:, 0]
    order = jnp.arange(tiles_here, dtype=jnp.int32)
    valid = order < tile_count[0]
    earlier = (dest[:, None] == dest[None, :]) & valid[None, :] & (order[None, :] < order[:, None])
    rank = jnp.sum(earlier.astype(jnp.int32), axis=1)
    slots = devices * capacity
    target = jnp.where(valid, dest * capacity + rank, slots)
    packed = jnp.concatenate(
        [
            voxel_offset.astype(jnp.float32)[:, None, :],
            fractions,
            normals,
            point_weight[:, None, :],
        ],
        axis=1,
    )
    outbox = jnp.zeros((slots, 8, tile_len), jnp.float32).at[target].set(packed, mode="drop")
    inbox = lax.all_to_all(outbox, ("gx", "yz"), split_axis=0, concat_axis=0, tiled=True)
    group = 16
    blocks = inbox.reshape(slots // group, group, 8, tile_len)
    plane = (BX + 2) * (BY + 2)
    start = (jnp.zeros((plane, BZ), jnp.float32), jnp.zeros((plane, BZ), jnp.float32))
    (rhs_acc, screen_acc), _ = lax.scan(splat_block, start, blocks)
    field = jnp.stack([rhs_acc, screen_acc]).reshape(2, BX + 2, BY + 2, BZ)
    from_below = passed_along(field[:, BX + 1], "gx", 1)
    from_above = passed_along(field[:, 0], "gx", -1)
    field = field.at[:, 1].add(from_below)
    field = field.at[:, BX].add(from_above)
    inner = field[:, 1 : BX + 1]
    from_left = passed_along(inner[:, :, BY + 1], "yz", 1)
    from_right = passed_along(inner[:, :, 0], "yz", -1)
    inner = inner.at[:, :, 1].add(from_left)
    inner = inner.at[:, :, BY].add(from_right)
    result = inner[:, :, 1 : BY + 1]
    return (result[0], result[1])


def solution(mesh):
    return jax.shard_map(
        shards,
        mesh=mesh,
        in_specs=(
            P(("gx", "yz"), None),
            P(("gx", "yz"), None),
            P(("gx", "yz"), None, None),
            P(("gx", "yz"), None, None),
            P(("gx", "yz"), None),
            P(("gx", "yz")),
        ),
        out_specs=(P("gx", "yz", None), P("gx", "yz", None)),
        check_vma=False,
    )
```

profile of v0, /device:TPU:7, one launch (start us, length us, event | category | flops | bytes accessed | tf_op | source)
XLA Modules:
  0.0 267.8 jit_solution(6114821710073582594)
XLA Ops:
  5.8 13.6 %scatter_fusion = f32[256,8,256]{2,1,0:T(8,128)} fusion(f32[256,8,256]{2,1,0:T(8,128)} %broadcast_in_dim.553, s32[128]{0:T(128)S(1)} %fusion.71, f32[128,8,256]{2,1,0:T(8,128)S(1)} %copy.17), kind=kCustom, calls=%fused_computation | custom fusion | bytes 3146240 | tf_op jit(solution)/shard_map/scatter | solution.py:92
  19.4 10.7 %all-to-all-start = ((f32[256,8,256]{2,1,0:T(8,128)}), f32[256,8,256]{2,1,0:T(8,128)S(1)}, u32[]{:S(2)}, u32[]{:S(2)}) async-start(f32[256,8,256]{2,1,0:T(8,128)} %scatter_fusion), calls=%async_computation | async-start | bytes 4194304 | tf_op jit(solution)/shard_map/all_to_all | solution.py:93
  30.2 29.3 %all-to-all-done = f32[256,8,256]{2,1,0:T(8,128)S(1)} async-done(((f32[256,8,256]{2,1,0:T(8,128)}), f32[256,8,256]{2,1,0:T(8,128)S(1)}, u32[]{:S(2)}, u32[]{:S(2)}) %all-to-all-start) | async-done | bytes 2097184 | tf_op jit(solution)/shard_map/all_to_all | solution.py:93
  59.5 188.7 %while.22 = (s32[]{:T(128)}, f32[60,128]{1,0:T(8,128)S(1)}, f32[60,128]{1,0:T(8,128)S(1)}, f32[16,16,8,256]{3,2,1,0:T(8,128)S(1)}, s32[]{:T(128)}, /*index=5*/s32[]{:T(128)}) while((s32[]{:T(128)}, f32[60,128]{1,0:T(8,128)S(1)}, f32[60,128]{1,0:T(8,128)S(1)}, f32[16,16,8,256]{3,2,1,0:T(8,128)S(1)}, s32[]{:T(128)}, ...), condition=%wide.region_3.4_spmd.clone, body=%wide.region_2.3_spmd.clone.sunk | while | flops 228026368 | bytes 8839260 | solution.py:98
  59.7 3.6 %convolution_add_fusion.2 = f32[60,128]{1,0:T(8,128)S(1)} fusion(f32[4096]{0:T(1024)S(1)} %get-tuple-element.440, f32[4096]{0:T(1024)S(1)} %get-tuple-element.441, f32[4096]{0:T(1024)S(1)} %get-tuple-element.442, f32[4096]{0:T(1024)S(1)} %get-tuple-element.443, f32[4096]{0:T(1024)S(1)} %get-tuple-element.444, f32[4096]{0:T(1024)S(1)} %get-tuple-element.445, ...), kind=kOutput, calls=%fused_computation.11.clone.1 | convolution fusion | flops 74284032 | bytes 454657 | tf_op jit(solution)/shard_map/while/body/eval_jaxpr/dot_general | solution.py:63
  65.2 5.5 %add_convert_fusion.14 = (bf16[4096,128]{1,0:T(8,128)(2,1)S(1)}, bf16[4096,128]{1,0:T(8,128)(2,1)S(1)}) fusion(f32[4096]{0:T(1024)S(1)} %get-tuple-element.403, s32[4096]{0:T(1024)S(1)} %get-tuple-element.405, f32[4096]{0:T(1024)S(1)} %get-tuple-element.406, s32[4096]{0:T(1024)S(1)} %get-tuple-element.407, f32[4096]{0:T(1024)S(1)} %get-tuple-element.408, ...), kind=kLoop, calls=%fused_computation.6.clone.2 | loop fusion | flops 7864320 | bytes 2244608 | tf_op jit(solution)/shard_map/while/body/eval_jaxpr/convert_element_type | solution.py:59
  71.5 3.6 %convolution_add_fusion.2 = f32[60,128]{1,0:T(8,128)S(1)} fusion(f32[4096]{0:T(1024)S(1)} %get-tuple-element.440, f32[4096]{0:T(1024)S(1)} %get-tuple-element.441, f32[4096]{0:T(1024)S(1)} %get-tuple-element.442, f32[4096]{0:T(1024)S(1)} %get-tuple-element.443, f32[4096]{0:T(1024)S(1)} %get-tuple-element.444, f32[4096]{0:T(1024)S(1)} %get-tuple-element.445, ...), kind=kOutput, calls=%fused_computation.11.clone.1 | convolution fusion | flops 74284032 | bytes 454657 | tf_op jit(solution)/shard_map/while/body/eval_jaxpr/dot_general | solution.py:63
  77.0 5.5 %add_convert_fusion.14 = (bf16[4096,128]{1,0:T(8,128)(2,1)S(1)}, bf16[4096,128]{1,0:T(8,128)(2,1)S(1)}) fusion(f32[4096]{0:T(1024)S(1)} %get-tuple-element.403, s32[4096]{0:T(1024)S(1)} %get-tuple-element.405, f32[4096]{0:T(1024)S(1)} %get-tuple-element.406, s32[4096]{0:T(1024)S(1)} %get-tuple-element.407, f32[4096]{0:T(1024)S(1)} %get-tuple-element.408, ...), kind=kLoop, calls=%fused_computation.6.clone.2 | loop fusion | flops 7864320 | bytes 2244608 | tf_op jit(solution)/shard_map/while/body/eval_jaxpr/convert_element_type | solution.py:59
  83.3 3.6 %convolution_add_fusion.2 = f32[60,128]{1,0:T(8,128)S(1)} fusion(f32[4096]{0:T(1024)S(1)} %get-tuple-element.440, f32[4096]{0:T(1024)S(1)} %get-tuple-element.441, f32[4096]{0:T(1024)S(1)} %get-tuple-element.442, f32[4096]{0:T(1024)S(1)} %get-tuple-element.443, f32[4096]{0:T(1024)S(1)} %get-tuple-element.444, f32[4096]{0:T(1024)S(1)} %get-tuple-element.445, ...), kind=kOutput, calls=%fused_computation.11.clone.1 | convolution fusion | flops 74284032 | bytes 454657 | tf_op jit(solution)/shard_map/while/body/eval_jaxpr/dot_general | solution.py:63
  88.8 5.5 %add_convert_fusion.14 = (bf16[4096,128]{1,0:T(8,128)(2,1)S(1)}, bf16[4096,128]{1,0:T(8,128)(2,1)S(1)}) fusion(f32[4096]{0:T(1024)S(1)} %get-tuple-element.403, s32[4096]{0:T(1024)S(1)} %get-tuple-element.405, f32[4096]{0:T(1024)S(1)} %get-tuple-element.406, s32[4096]{0:T(1024)S(1)} %get-tuple-element.407, f32[4096]{0:T(1024)S(1)} %get-tuple-element.408, ...), kind=kLoop, calls=%fused_computation.6.clone.2 | loop fusion | flops 7864320 | bytes 2244608 | tf_op jit(solution)/shard_map/while/body/eval_jaxpr/convert_element_type | solution.py:59
  95.1 3.6 %convolution_add_fusion.2 = f32[60,128]{1,0:T(8,128)S(1)} fusion(f32[4096]{0:T(1024)S(1)} %get-tuple-element.440, f32[4096]{0:T(1024)S(1)} %get-tuple-element.441, f32[4096]{0:T(1024)S(1)} %get-tuple-element.442, f32[4096]{0:T(1024)S(1)} %get-tuple-element.443, f32[4096]{0:T(1024)S(1)} %get-tuple-element.444, f32[4096]{0:T(1024)S(1)} %get-tuple-element.445, ...), kind=kOutput, calls=%fused_computation.11.clone.1 | convolution fusion | flops 74284032 | bytes 454657 | tf_op jit(solution)/shard_map/while/body/eval_jaxpr/dot_general | solution.py:63
  100.6 5.5 %add_convert_fusion.14 = (bf16[4096,128]{1,0:T(8,128)(2,1)S(1)}, bf16[4096,128]{1,0:T(8,128)(2,1)S(1)}) fusion(f32[4096]{0:T(1024)S(1)} %get-tuple-element.403, s32[4096]{0:T(1024)S(1)} %get-tuple-element.405, f32[4096]{0:T(1024)S(1)} %get-tuple-element.406, s32[4096]{0:T(1024)S(1)} %get-tuple-element.407, f32[4096]{0:T(1024)S(1)} %get-tuple-element.408, ...), kind=kLoop, calls=%fused_computation.6.clone.2 | loop fusion | flops 7864320 | bytes 2244608 | tf_op jit(solution)/shard_map/while/body/eval_jaxpr/convert_element_type | solution.py:59
  106.9 3.6 %convolution_add_fusion.2 = f32[60,128]{1,0:T(8,128)S(1)} fusion(f32[4096]{0:T(1024)S(1)} %get-tuple-element.440, f32[4096]{0:T(1024)S(1)} %get-tuple-element.441, f32[4096]{0:T(1024)S(1)} %get-tuple-element.442, f32[4096]{0:T(1024)S(1)} %get-tuple-element.443, f32[4096]{0:T(1024)S(1)} %get-tuple-element.444, f32[4096]{0:T(1024)S(1)} %get-tuple-element.445, ...), kind=kOutput, calls=%fused_computation.11.clone.1 | convolution fusion | flops 74284032 | bytes 454657 | tf_op jit(solution)/shard_map/while/body/eval_jaxpr/dot_general | solution.py:63
  112.4 5.5 %add_convert_fusion.14 = (bf16[4096,128]{1,0:T(8,128)(2,1)S(1)}, bf16[4096,128]{1,0:T(8,128)(2,1)S(1)}) fusion(f32[4096]{0:T(1024)S(1)} %get-tuple-element.403, s32[4096]{0:T(1024)S(1)} %get-tuple-element.405, f32[4096]{0:T(1024)S(1)} %get-tuple-element.406, s32[4096]{0:T(1024)S(1)} %get-tuple-element.407, f32[4096]{0:T(1024)S(1)} %get-tuple-element.408, ...), kind=kLoop, calls=%fused_computation.6.clone.2 | loop fusion | flops 7864320 | bytes 2244608 | tf_op jit(solution)/shard_map/while/body/eval_jaxpr/convert_element_type | solution.py:59
  118.7 3.6 %convolution_add_fusion.2 = f32[60,128]{1,0:T(8,128)S(1)} fusion(f32[4096]{0:T(1024)S(1)} %get-tuple-element.440, f32[4096]{0:T(1024)S(1)} %get-tuple-element.441, f32[4096]{0:T(1024)S(1)} %get-tuple-element.442, f32[4096]{0:T(1024)S(1)} %get-tuple-element.443, f32[4096]{0:T(1024)S(1)} %get-tuple-element.444, f32[4096]{0:T(1024)S(1)} %get-tuple-element.445, ...), kind=kOutput, calls=%fused_computation.11.clone.1 | convolution fusion | flops 74284032 | bytes 454657 | tf_op jit(solution)/shard_map/while/body/eval_jaxpr/dot_general | solution.py:63
  124.2 5.5 %add_convert_fusion.14 = (bf16[4096,128]{1,0:T(8,128)(2,1)S(1)}, bf16[4096,128]{1,0:T(8,128)(2,1)S(1)}) fusion(f32[4096]{0:T(1024)S(1)} %get-tuple-element.403, s32[4096]{0:T(1024)S(1)} %get-tuple-element.405, f32[4096]{0:T(1024)S(1)} %get-tuple-element.406, s32[4096]{0:T(1024)S(1)} %get-tuple-element.407, f32[4096]{0:T(1024)S(1)} %get-tuple-element.408, ...), kind=kLoop, calls=%fused_computation.6.clone.2 | loop fusion | flops 7864320 | bytes 2244608 | tf_op jit(solution)/shard_map/while/body/eval_jaxpr/convert_element_type | solution.py:59
  130.5 3.6 %convolution_add_fusion.2 = f32[60,128]{1,0:T(8,128)S(1)} fusion(f32[4096]{0:T(1024)S(1)} %get-tuple-element.440, f32[4096]{0:T(1024)S(1)} %get-tuple-element.441, f32[4096]{0:T(1024)S(1)} %get-tuple-element.442, f32[4096]{0:T(1024)S(1)} %get-tuple-element.443, f32[4096]{0:T(1024)S(1)} %get-tuple-element.444, f32[4096]{0:T(1024)S(1)} %get-tuple-element.445, ...), kind=kOutput, calls=%fused_computation.11.clone.1 | convolution fusion | flops 74284032 | bytes 454657 | tf_op jit(solution)/shard_map/while/body/eval_jaxpr/dot_general | solution.py:63
  136.0 5.5 %add_convert_fusion.14 = (bf16[4096,128]{1,0:T(8,128)(2,1)S(1)}, bf16[4096,128]{1,0:T(8,128)(2,1)S(1)}) fusion(f32[4096]{0:T(1024)S(1)} %get-tuple-element.403, s32[4096]{0:T(1024)S(1)} %get-tuple-element.405, f32[4096]{0:T(1024)S(1)} %get-tuple-element.406, s32[4096]{0:T(1024)S(1)} %get-tuple-element.407, f32[4096]{0:T(1024)S(1)} %get-tuple-element.408, ...), kind=kLoop, calls=%fused_computation.6.clone.2 | loop fusion | flops 7864320 | bytes 2244608 | tf_op jit(solution)/shard_map/while/body/eval_jaxpr/convert_element_type | solution.py:59
  142.3 3.6 %convolution_add_fusion.2 = f32[60,128]{1,0:T(8,128)S(1)} fusion(f32[4096]{0:T(1024)S(1)} %get-tuple-element.440, f32[4096]{0:T(1024)S(1)} %get-tuple-element.441, f32[4096]{0:T(1024)S(1)} %get-tuple-element.442, f32[4096]{0:T(1024)S(1)} %get-tuple-element.443, f32[4096]{0:T(1024)S(1)} %get-tuple-element.444, f32[4096]{0:T(1024)S(1)} %get-tuple-element.445, ...), kind=kOutput, calls=%fused_computation.11.clone.1 | convolution fusion | flops 74284032 | bytes 454657 | tf_op jit(solution)/shard_map/while/body/eval_jaxpr/dot_general | solution.py:63
  147.7 5.5 %add_convert_fusion.14 = (bf16[4096,128]{1,0:T(8,128)(2,1)S(1)}, bf16[4096,128]{1,0:T(8,128)(2,1)S(1)}) fusion(f32[4096]{0:T(1024)S(1)} %get-tuple-element.403, s32[4096]{0:T(1024)S(1)} %get-tuple-element.405, f32[4096]{0:T(1024)S(1)} %get-tuple-element.406, s32[4096]{0:T(1024)S(1)} %get-tuple-element.407, f32[4096]{0:T(1024)S(1)} %get-tuple-element.408, ...), kind=kLoop, calls=%fused_computation.6.clone.2 | loop fusion | flops 7864320 | bytes 2244608 | tf_op jit(solution)/shard_map/while/body/eval_jaxpr/convert_element_type | solution.py:59
  154.1 3.6 %convolution_add_fusion.2 = f32[60,128]{1,0:T(8,128)S(1)} fusion(f32[4096]{0:T(1024)S(1)} %get-tuple-element.440, f32[4096]{0:T(1024)S(1)} %get-tuple-element.441, f32[4096]{0:T(1024)S(1)} %get-tuple-element.442, f32[4096]{0:T(1024)S(1)} %get-tuple-element.443, f32[4096]{0:T(1024)S(1)} %get-tuple-element.444, f32[4096]{0:T(1024)S(1)} %get-tuple-element.445, ...), kind=kOutput, calls=%fused_computation.11.clone.1 | convolution fusion | flops 74284032 | bytes 454657 | tf_op jit(solution)/shard_map/while/body/eval_jaxpr/dot_general | solution.py:63
  159.5 5.5 %add_convert_fusion.14 = (bf16[4096,128]{1,0:T(8,128)(2,1)S(1)}, bf16[4096,128]{1,0:T(8,128)(2,1)S(1)}) fusion(f32[4096]{0:T(1024)S(1)} %get-tuple-element.403, s32[4096]{0:T(1024)S(1)} %get-tuple-element.405, f32[4096]{0:T(1024)S(1)} %get-tuple-element.406, s32[4096]{0:T(1024)S(1)} %get-tuple-element.407, f32[4096]{0:T(1024)S(1)} %get-tuple-element.408, ...), kind=kLoop, calls=%fused_computation.6.clone.2 | loop fusion | flops 7864320 | bytes 2244608 | tf_op jit(solution)/shard_map/while/body/eval_jaxpr/convert_element_type | solution.py:59
  171.3 5.5 %add_convert_fusion.14 = (bf16[4096,128]{1,0:T(8,128)(2,1)S(1)}, bf16[4096,128]{1,0:T(8,128)(2,1)S(1)}) fusion(f32[4096]{0:T(1024)S(1)} %get-tuple-element.403, s32[4096]{0:T(1024)S(1)} %get-tuple-element.405, f32[4096]{0:T(1024)S(1)} %get-tuple-element.406, s32[4096]{0:T(1024)S(1)} %get-tuple-element.407, f32[4096]{0:T(1024)S(1)} %get-tuple-element.408, ...), kind=kLoop, calls=%fused_computation.6.clone.2 | loop fusion | flops 7864320 | bytes 2244608 | tf_op jit(solution)/shard_map/while/body/eval_jaxpr/convert_element_type | solution.py:59
  177.7 3.6 %convolution_add_fusion.2 = f32[60,128]{1,0:T(8,128)S(1)} fusion(f32[4096]{0:T(1024)S(1)} %get-tuple-element.440, f32[4096]{0:T(1024)S(1)} %get-tuple-element.441, f32[4096]{0:T(1024)S(1)} %get-tuple-element.442, f32[4096]{0:T(1024)S(1)} %get-tuple-element.443, f32[4096]{0:T(1024)S(1)} %get-tuple-element.444, f32[4096]{0:T(1024)S(1)} %get-tuple-element.445, ...), kind=kOutput, calls=%fused_computation.11.clone.1 | convolution fusion | flops 74284032 | bytes 454657 | tf_op jit(solution)/shard_map/while/body/eval_jaxpr/dot_general | solution.py:63
  183.1 5.5 %add_convert_fusion.14 = (bf16[4096,128]{1,0:T(8,128)(2,1)S(1)}, bf16[4096,128]{1,0:T(8,128)(2,1)S(1)}) fusion(f32[4096]{0:T(1024)S(1)} %get-tuple-element.403, s32[4096]{0:T(1024)S(1)} %get-tuple-element.405, f32[4096]{0:T(1024)S(1)} %get-tuple-element.406, s32[4096]{0:T(1024)S(1)} %get-tuple-element.407, f32[4096]{0:T(1024)S(1)} %get-tuple-element.408, ...), kind=kLoop, calls=%fused_computation.6.clone.2 | loop fusion | flops 7864320 | bytes 2244608 | tf_op jit(solution)/shard_map/while/body/eval_jaxpr/convert_element_type | solution.py:59
  194.9 5.5 %add_convert_fusion.14 = (bf16[4096,128]{1,0:T(8,128)(2,1)S(1)}, bf16[4096,128]{1,0:T(8,128)(2,1)S(1)}) fusion(f32[4096]{0:T(1024)S(1)} %get-tuple-element.403, s32[4096]{0:T(1024)S(1)} %get-tuple-element.405, f32[4096]{0:T(1024)S(1)} %get-tuple-element.406, s32[4096]{0:T(1024)S(1)} %get-tuple-element.407, f32[4096]{0:T(1024)S(1)} %get-tuple-element.408, ...), kind=kLoop, calls=%fused_computation.6.clone.2 | loop fusion | flops 7864320 | bytes 2244608 | tf_op jit(solution)/shard_map/while/body/eval_jaxpr/convert_element_type | solution.py:59
  206.7 5.5 %add_convert_fusion.14 = (bf16[4096,128]{1,0:T(8,128)(2,1)S(1)}, bf16[4096,128]{1,0:T(8,128)(2,1)S(1)}) fusion(f32[4096]{0:T(1024)S(1)} %get-tuple-element.403, s32[4096]{0:T(1024)S(1)} %get-tuple-element.405, f32[4096]{0:T(1024)S(1)} %get-tuple-element.406, s32[4096]{0:T(1024)S(1)} %get-tuple-element.407, f32[4096]{0:T(1024)S(1)} %get-tuple-element.408, ...), kind=kLoop, calls=%fused_computation.6.clone.2 | loop fusion | flops 7864320 | bytes 2244608 | tf_op jit(solution)/shard_map/while/body/eval_jaxpr/convert_element_type | solution.py:59
  213.0 3.6 %convolution_add_fusion.2 = f32[60,128]{1,0:T(8,128)S(1)} fusion(f32[4096]{0:T(1024)S(1)} %get-tuple-element.440, f32[4096]{0:T(1024)S(1)} %get-tuple-element.441, f32[4096]{0:T(1024)S(1)} %get-tuple-element.442, f32[4096]{0:T(1024)S(1)} %get-tuple-element.443, f32[4096]{0:T(1024)S(1)} %get-tuple-element.444, f32[4096]{0:T(1024)S(1)} %get-tuple-element.445, ...), kind=kOutput, calls=%fused_computation.11.clone.1 | convolution fusion | flops 74284032 | bytes 454657 | tf_op jit(solution)/shard_map/while/body/eval_jaxpr/dot_general | solution.py:63
  218.5 5.5 %add_convert_fusion.14 = (bf16[4096,128]{1,0:T(8,128)(2,1)S(1)}, bf16[4096,128]{1,0:T(8,128)(2,1)S(1)}) fusion(f32[4096]{0:T(1024)S(1)} %get-tuple-element.403, s32[4096]{0:T(1024)S(1)} %get-tuple-element.405, f32[4096]{0:T(1024)S(1)} %get-tuple-element.406, s32[4096]{0:T(1024)S(1)} %get-tuple-element.407, f32[4096]{0:T(1024)S(1)} %get-tuple-element.408, ...), kind=kLoop, calls=%fused_computation.6.clone.2 | loop fusion | flops 7864320 | bytes 2244608 | tf_op jit(solution)/shard_map/while/body/eval_jaxpr/convert_element_type | solution.py:59
  230.3 5.5 %add_convert_fusion.14 = (bf16[4096,128]{1,0:T(8,128)(2,1)S(1)}, bf16[4096,128]{1,0:T(8,128)(2,1)S(1)}) fusion(f32[4096]{0:T(1024)S(1)} %get-tuple-element.403, s32[4096]{0:T(1024)S(1)} %get-tuple-element.405, f32[4096]{0:T(1024)S(1)} %get-tuple-element.406, s32[4096]{0:T(1024)S(1)} %get-tuple-element.407, f32[4096]{0:T(1024)S(1)} %get-tuple-element.408, ...), kind=kLoop, calls=%fused_computation.6.clone.2 | loop fusion | flops 7864320 | bytes 2244608 | tf_op jit(solution)/shard_map/while/body/eval_jaxpr/convert_element_type | solution.py:59
  242.1 5.5 %add_convert_fusion.14 = (bf16[4096,128]{1,0:T(8,128)(2,1)S(1)}, bf16[4096,128]{1,0:T(8,128)(2,1)S(1)}) fusion(f32[4096]{0:T(1024)S(1)} %get-tuple-element.403, s32[4096]{0:T(1024)S(1)} %get-tuple-element.405, f32[4096]{0:T(1024)S(1)} %get-tuple-element.406, s32[4096]{0:T(1024)S(1)} %get-tuple-element.407, f32[4096]{0:T(1024)S(1)} %get-tuple-element.408, ...), kind=kLoop, calls=%fused_computation.6.clone.2 | loop fusion | flops 7864320 | bytes 2244608 | tf_op jit(solution)/shard_map/while/body/eval_jaxpr/convert_element_type | solution.py:59
  262.7 4.5 %collective-permute-done.3 = f32[2,4,128]{2,1,0:T(4,128)S(1)} collective-permute-done((f32[2,4,128]{2,1,0:T(4,128)S(1)}, f32[2,4,128]{2,1,0:T(4,128)S(1)}, u32[]{:S(2)}, u32[]{:S(2)}) %collective-permute-start.3) | collective-permute-done | bytes 4128 | tf_op jit(solution)/shard_map/ppermute | solution.py:14
  (184 shorter events, 78.6 us)
Async XLA Ops:
  2.2 1.9 copy-start
  19.4 40.0 %all-to-all-start = ((f32[256,8,256]{2,1,0:T(8,128)}), f32[256,8,256]{2,1,0:T(8,128)S(1)}, u32[]{:S(2)}, u32[]{:S(2)}) async-start(f32[256,8,256]{2,1,0:T(8,128)} %scatter_fusion), calls=%async_computation | async-start | bytes 4194304 | tf_op jit(solution)/shard_map/all_to_all | solution.py:93
  248.2 3.2 %collective-permute-start = (f32[2,10,128]{2,0,1:T(2,128)S(1)}, f32[2,10,128]{2,0,1:T(2,128)S(1)}, u32[]{:S(2)}, u32[]{:S(2)}) collective-permute-start(f32[2,10,128]{2,0,1:T(2,128)S(1)} %fusion.69), channel_id=1, source_target_pairs={{0,16},{16,32},{32,48},{48,64},{64,80},{80,96},{96,112},{1,17},{17... | collective-permute-start | bytes 30728 | tf_op jit(solution)/shard_map/ppermute | solution.py:14
  251.5 5.5 %collective-permute-start.1 = (f32[2,10,128]{2,0,1:T(2,128)S(1)}, f32[2,10,128]{2,0,1:T(2,128)S(1)}, u32[]{:S(2)}, u32[]{:S(2)}) collective-permute-start(f32[2,10,128]{2,0,1:T(2,128)S(1)} %get-tuple-element.316), channel_id=1, source_target_pairs={{16,0},{32,16},{48,32},{64,48},{80,64},{96,80},{112,96},{17,1},{33... | collective-permute-start | bytes 30728 | tf_op jit(solution)/shard_map/ppermute | solution.py:14
  257.1 5.5 %collective-permute-start.2 = (f32[2,4,128]{2,1,0:T(4,128)S(1)}, f32[2,4,128]{2,1,0:T(4,128)S(1)}, u32[]{:S(2)}, u32[]{:S(2)}) collective-permute-start(f32[2,4,128]{2,1,0:T(4,128)S(1)} %get-tuple-element.313), channel_id=1, source_target_pairs={{0,1},{1,2},{2,3},{3,4},{4,5},{5,6},{6,7},{7,8},{8,9},{9,10},{10,1... | collective-permute-start | bytes 12296 | tf_op jit(solution)/shard_map/ppermute | solution.py:14
  260.7 6.5 %collective-permute-start.3 = (f32[2,4,128]{2,1,0:T(4,128)S(1)}, f32[2,4,128]{2,1,0:T(4,128)S(1)}, u32[]{:S(2)}, u32[]{:S(2)}) collective-permute-start(f32[2,4,128]{2,1,0:T(4,128)S(1)} %get-tuple-element.312), channel_id=1, source_target_pairs={{1,0},{2,1},{3,2},{4,3},{5,4},{6,5},{7,6},{8,7},{9,8},{10,9},{11,1... | collective-permute-start | bytes 12296 | tf_op jit(solution)/shard_map/ppermute | solution.py:14
where the time goes:
time: 269 us; the launch traced here: 268 us
  other arithmetic  124 us (46%)
  matrix products  66 us (25%)
  waiting for transfers between devices  38 us (14%)
  starting transfers between devices  20.5 us (8%)
  local copies, waits for them, and re-layouts  16.8 us (6%)
    convert_element_type x16, other arithmetic, splat_block(): z_value = z_value.astype(jnp.bfloat16)  88.3 us
    dot_general x16, matrix products, splat_block(): jnp.dot(a_screen.astype(jnp.bfloat16), z_value, preferred_element_type=jn...  58 us
    all_to_all x1, waiting for transfers between devices, shards(): lax.all_to_all(outbox, ('gx', 'yz'), split_axis=0, concat_axis=0, tiled=T...  29.3 us
    another operation x32, other arithmetic  29.1 us
    scatter x1, local copies, waits for them, and re-layouts, shards(): jnp.zeros((slots, 8, tile_len), jnp.float32).at[target]  13.6 us
    all_to_all x1, starting transfers between devices, shards(): lax.all_to_all(outbox, ('gx', 'yz'), split_axis=0, concat_axis=0, tiled=T...  10.7 us
    ppermute x4, starting transfers between devices, passed_along(): lax.ppermute(value, axis, [(source, source + steps) for source in range(f...  9.79 us
    ppermute x4, waiting for transfers between devices, passed_along(): lax.ppermute(value, axis, [(source, source + steps) for source in range(f...  8.79 us
  transfers between devices with their start and end apart: 5, of which 4 were waited for; matrix products, arithmetic and copies ran while one was open for 0% of the time, Pallas kernels for 0%

commit v1 on v0

v1 whole, which is shorter than its diff:
```python
import jax
import jax.numpy as jnp
from jax import lax
from jax.experimental import pallas as pl
from jax.experimental.pallas import tpu as pltpu
from jax.sharding import PartitionSpec as P

BX = 4
BY = 8
BZ = 128
CAP = 2
ROWS = 8 * (BY + 2)
GROUP = 4


def passed_along(value, axis, steps):
    count = lax.axis_size(axis)
    first, last = (max(0, -steps), min(count, count - steps))
    return lax.ppermute(value, axis, [(source, source + steps) for source in range(first, last)])


def dispatch_kernel(ids_ref, count_ref, offset_ref, frac_ref, normal_ref, weight_ref, out_ref, seen_ref):
    slots = out_ref.shape[0]

    def clear(i, _):
        out_ref[pl.ds(i * 8, 8)] = jnp.zeros((8,) + out_ref.shape[1:], jnp.float32)
        return 0

    lax.fori_loop(0, slots // 8, clear, 0)

    def reset(i, _):
        seen_ref[i] = 0
        return 0

    lax.fori_loop(0, seen_ref.shape[0], reset, 0)

    def place(t, _):
        brick = ids_ref[t]
        rank = seen_ref[brick]
        seen_ref[brick] = rank + 1
        slot = brick * CAP + jnp.minimum(rank, CAP - 1)
        out_ref[slot, 0:3, :] = frac_ref[t]
        out_ref[slot, 3:4, :] = offset_ref[pl.ds(t, 1), :].astype(jnp.float32)
        out_ref[slot, 4:7, :] = normal_ref[t]
        out_ref[slot, 7:8, :] = weight_ref[pl.ds(t, 1), :]
        return 0

    lax.fori_loop(0, jnp.minimum(count_ref[0], ids_ref.shape[0]), place, 0)


def dispatch(ids, count, offset, frac, normal, weight, bricks):
    smem = pl.BlockSpec(memory_space=pltpu.SMEM)
    vmem = pl.BlockSpec(memory_space=pltpu.VMEM)
    return pl.pallas_call(
        dispatch_kernel,
        out_shape=jax.ShapeDtypeStruct((bricks * CAP, 8, offset.shape[1]), jnp.float32),
        in_specs=[smem, smem, vmem, vmem, vmem, vmem],
        out_specs=vmem,
        scratch_shapes=[pltpu.SMEM((bricks,), jnp.int32)],
        name="dispatch",
    )(ids, count, offset, frac, normal, weight)


def bspline(t):
    outer = jnp.maximum(1.5 - jnp.abs(t), 0.0)
    inner = jnp.maximum(outer - 1.0, 0.0)
    value = outer * outer - 3.0 * (inner * inner)
    slope = jnp.minimum(jnp.maximum(t + t, -outer), outer)
    return value, slope


def build(inbox_ref, tile, lanes, y_ref, a_ref, z_ref, col):
    def row(c):
        return jnp.broadcast_to(inbox_ref[tile, c : c + 1, lanes], (8, 128))

    sub = lax.broadcasted_iota(jnp.int32, (8, 128), 0).astype(jnp.float32)
    offset = row(3).astype(jnp.int32)
    cell_x = lax.shift_right_logical(offset, 10).astype(jnp.float32)
    cell_y = (lax.shift_right_logical(offset, 7) & 7).astype(jnp.float32)
    cell_z = (offset & 127).astype(jnp.float32)
    x_value, x_slope = bspline((sub - 0.5) - (cell_x + row(0)))
    at_y = cell_y + row(1)
    for half in range(2):
        y_value, y_slope = bspline((sub + (8 * half - 0.5)) - at_y)
        y_ref[8 * half : 8 * half + 8, :] = y_value
        y_ref[16 + 8 * half : 24 + 8 * half, :] = y_slope
    one = row(4) * x_slope
    two = row(5) * x_value
    three = row(6) * x_value
    screen = row(7) * x_value
    cols = pl.ds(col, 128)
    for pair in range((BY + 2) // 2):
        planes = [[], [], []]
        for s in (2 * pair, 2 * pair + 1):
            yv = jnp.broadcast_to(y_ref[s : s + 1, :], (8, 128))
            ys = jnp.broadcast_to(y_ref[16 + s : 17 + s, :], (8, 128))
            planes[0].append(one * yv + two * ys)
            planes[1].append(three * yv)
            planes[2].append(screen * yv)
        for k in range(3):
            a_ref[k * ROWS + 16 * pair : k * ROWS + 16 * pair + 16, cols] = jnp.concatenate(
                planes[k], axis=0
            ).astype(jnp.bfloat16)
    fz = row(2)

    def half_row(v):
        return jnp.concatenate([v, v], axis=0).astype(jnp.bfloat16)

    weights = [half_row(0.5 * (1.0 - fz) * (1.0 - fz)), half_row(0.75 - (fz - 0.5) * (fz - 0.5)), half_row(0.5 * fz * fz)]
    slopes = [half_row(fz - 1.0), half_row(1.0 - 2.0 * fz), half_row(fz)]
    where = [half_row(cell_z - 1.0), half_row(cell_z), half_row(cell_z + 1.0)]
    zero = jnp.zeros((16, 128), jnp.bfloat16)
    depth = lax.broadcasted_iota(jnp.int32, (16, 128), 0).astype(jnp.float32)
    for block in range(BZ // 16):
        here = (depth + 16.0 * block).astype(jnp.bfloat16)
        hits = [here == w for w in where]
        value = jnp.where(hits[0], weights[0], jnp.where(hits[1], weights[1], jnp.where(hits[2], weights[2], zero)))
        slope = jnp.where(hits[0], slopes[0], jnp.where(hits[1], slopes[1], jnp.where(hits[2], slopes[2], zero)))
        z_ref[16 * block : 16 * block + 16, cols] = value
        z_ref[BZ + 16 * block : BZ + 16 * block + 16, cols] = slope


def splat_kernel(inbox_ref, out_ref, acc_ref, y_ref, a0, z0, a1, z1):
    slots, _, points = inbox_ref.shape
    steps = slots // GROUP

    def fill(step, a_ref, z_ref):
        for g in range(GROUP):
            for h in range(points // 128):
                build(inbox_ref, step * GROUP + g, pl.ds(128 * h, 128), y_ref, a_ref, z_ref, g * points + 128 * h)

    def product(a_ref, z_ref):
        acc_ref[...] += lax.dot_general(
            a_ref[...], z_ref[...], (((1,), (1,)), ((), ())), preferred_element_type=jnp.float32
        )

    acc_ref[...] = jnp.zeros_like(acc_ref)
    fill(0, a0, z0)

    def body(i, _):
        product(a0, z0)
        fill(2 * i + 1, a1, z1)
        product(a1, z1)
        fill(jnp.minimum(2 * i + 2, steps - 1), a0, z0)
        return 0

    lax.fori_loop(0, steps // 2, body, 0)
    out_ref[0] = 0.5 * acc_ref[0:ROWS, 0:BZ] + 0.25 * acc_ref[ROWS : 2 * ROWS, BZ : 2 * BZ]
    out_ref[1] = 0.25 * acc_ref[2 * ROWS : 3 * ROWS, 0:BZ]


def splat(inbox):
    points = inbox.shape[2]
    width = GROUP * points
    vmem = pl.BlockSpec(memory_space=pltpu.VMEM)
    return pl.pallas_call(
        splat_kernel,
        out_shape=jax.ShapeDtypeStruct((2, ROWS, BZ), jnp.float32),
        in_specs=[vmem],
        out_specs=vmem,
        scratch_shapes=[
            pltpu.VMEM((3 * ROWS, 2 * BZ), jnp.float32),
            pltpu.VMEM((32, 128), jnp.float32),
            pltpu.VMEM((3 * ROWS, width), jnp.bfloat16),
            pltpu.VMEM((2 * BZ, width), jnp.bfloat16),
            pltpu.VMEM((3 * ROWS, width), jnp.bfloat16),
            pltpu.VMEM((2 * BZ, width), jnp.bfloat16),
        ],
        name="splat",
    )(inbox)


def shards(brick_ids, voxel_offset, fractions, normals, point_weight, tile_count):
    bricks = lax.axis_size("gx") * lax.axis_size("yz")
    outbox = dispatch(brick_ids[:, 0], tile_count, voxel_offset, fractions, normals, point_weight, bricks)
    inbox = lax.all_to_all(outbox, ("gx", "yz"), split_axis=0, concat_axis=0, tiled=True)
    field = splat(inbox).reshape(2, BY + 2, 8, BZ)
    from_below = passed_along(field[:, :, BX + 1], "gx", 1)
    from_above = passed_along(field[:, :, 0], "gx", -1)
    rows = [field[:, :, r] for r in range(1, BX + 1)]
    rows[0] = rows[0] + from_below
    rows[-1] = rows[-1] + from_above
    inner = jnp.stack(rows, axis=1)
    from_left = passed_along(inner[:, :, BY + 1], "yz", 1)
    from_right = passed_along(inner[:, :, 0], "yz", -1)
    middle = inner[:, :, 1 : BY + 1]
    left = jnp.pad(from_left[:, :, None], ((0, 0), (0, 0), (0, BY - 1), (0, 0)))
    right = jnp.pad(from_right[:, :, None], ((0, 0), (0, 0), (BY - 1, 0), (0, 0)))
    result = middle + left + right
    return (result[0], result[1])


def solution(mesh):
    return jax.shard_map(
        shards,
        mesh=mesh,
        in_specs=(
            P(("gx", "yz"), None),
            P(("gx", "yz"), None),
            P(("gx", "yz"), None, None),
            P(("gx", "yz"), None, None),
            P(("gx", "yz"), None),
            P(("gx", "yz")),
        ),
        out_specs=(P("gx", "yz", None), P("gx", "yz", None)),
        check_vma=False,
    )
```

time: 269 us -> 108 us (0.40)
  the two profiles are of different devices: /device:TPU:7 before, /device:TPU:38 now
where the time goes in v1:
time: 108 us; the launch traced here: 107 us
  Pallas kernels  41.9 us (39%)
  blocking collectives  38.4 us (36%)
  starting transfers between devices  10.8 us (10%)
  waiting for transfers between devices  8.32 us (8%)
  local copies, waits for them, and re-layouts  6.14 us (6%)
  between operations  1.4 us (1%)
    all_to_all x1, blocking collectives, shards(): lax.all_to_all(outbox, ('gx', 'yz'), split_axis=0, concat_axis=0, tiled=T...  38.4 us
    pallas_call x1, Pallas kernels, splat(): pl.pallas_call(splat_kernel, out_shape=jax.ShapeDtypeStruct((2, ROWS, BZ)...  36.9 us
    ppermute x4, starting transfers between devices, passed_along(): lax.ppermute(value, axis, [(source, source + steps) for source in range(f...  10.8 us
    ppermute x4, waiting for transfers between devices, passed_along(): lax.ppermute(value, axis, [(source, source + steps) for source in range(f...  8.32 us
    pallas_call x1, Pallas kernels, dispatch(): pl.pallas_call(dispatch_kernel, out_shape=jax.ShapeDtypeStruct((bricks *...  4.98 us
    unnamed x6, local copies, waits for them, and re-layouts  4.18 us
  transfers between devices with their start and end apart: 4, of which 2 were waited for; matrix products, arithmetic and copies ran while one was open for 0% of the time, Pallas kernels for 0%

profile of v1, /device:TPU:38, one launch (start us, length us, event | category | flops | bytes accessed | tf_op | source)
XLA Modules:
  0.0 107.1 jit_solution(17123219081034839014)
XLA Ops:
  1.3 2.1 %copy.8.frac_ref = f32[128,3,256]{2,1,0:T(4,128)} copy(f32[128,3,256]{2,0,1:T(8,128)} %param.8) | data formatting | bytes 786432 | tf_op args[2]
  3.3 2.1 %copy.9.normal_ref = f32[128,3,256]{2,1,0:T(4,128)} copy(f32[128,3,256]{2,0,1:T(8,128)} %param.9) | data formatting | bytes 786432 | tf_op args[3]
  5.4 5.0 %dispatch.1 = f32[256,8,256]{2,1,0:T(8,128)} custom-call(s32[128]{0:T(128)} %bitcast.43, s32[1]{0:T(128)S(6)} %copy.34.count_ref, s32[128,256]{1,0:T(8,128)} %offset_ref.1, f32[128,3,256]{2,1,0:T(4,128)} %copy.8.frac_ref, f32[128,3,256]{2,1,0:T(4,128)} %copy.9.normal_ref, f32[128,256]{1,0:T(8,128)} %weight_ref.1), custom_call_target="tpu_custom_call" | custom-call | tf_op jit(solution)/shard_map/dispatch/pallas_call | solution.py:54
  10.4 38.4 %all_to_all.5.inbox_ref = f32[256,8,256]{2,1,0:T(8,128)} all-to-all(f32[256,8,256]{2,1,0:T(8,128)} %dispatch.1), channel_id=1, replica_groups=mesh['gx'=8,'yz'=16] {'gx','yz'}, dimensions={0} | all-to-all | bytes 4194304 | tf_op jit(solution)/shard_map/all_to_all | solution.py:176
  48.8 36.9 %splat.1 = f32[2,80,128]{2,1,0:T(8,128)} custom-call(f32[256,8,256]{2,1,0:T(8,128)} %all_to_all.5.inbox_ref), custom_call_target="tpu_custom_call" | custom-call | tf_op jit(solution)/shard_map/splat/pallas_call | solution.py:156
  85.7 1.4 %fusion.2 = (f32[2,10,1,128]{3,2,1,0:T(1,128)S(1)}, f32[2,10,1,128]{3,2,1,0:T(1,128)S(1)}, f32[2,10,1,128]{3,2,1,0:T(1,128)S(1)}, f32[2,10,1,128]{3,2,1,0:T(1,12...) fusion(f32[2,10,8,128]{3,2,1,0:T(8,128)} %bitcast.30), kind=kLoop, calls=%fused_computation.13 | loop fusion | bytes 122880 | tf_op jit(solution)/shard_map/slice | solution.py:180
  87.1 3.1 %collective-permute-start.1 = (f32[2,10,128]{2,0,1:T(2,128)S(1)}, f32[2,10,128]{2,0,1:T(2,128)S(1)}, u32[]{:S(2)}, u32[]{:S(2)}) collective-permute-start(f32[2,10,128]{2,0,1:T(2,128)S(1)} %bitcast.39), channel_id=1, source_target_pairs={{16,0},{32,16},{48,32},{64,48},{80,64},{96,80},{112,96},{17,1},{33... | collective-permute-start | bytes 30728 | tf_op jit(solution)/shard_map/ppermute | solution.py:19
  90.2 1.9 %collective-permute-start = (f32[2,10,128]{2,0,1:T(2,128)S(1)}, f32[2,10,128]{2,0,1:T(2,128)S(1)}, u32[]{:S(2)}, u32[]{:S(2)}) collective-permute-start(f32[2,10,128]{2,0,1:T(2,128)S(1)} %bitcast.40), channel_id=1, source_target_pairs={{0,16},{16,32},{32,48},{48,64},{64,80},{80,96},{96,112},{1,17},{17... | collective-permute-start | bytes 30728 | tf_op jit(solution)/shard_map/ppermute | solution.py:19
  92.1 0.0 collective-permute-done.1
  92.2 3.0 %collective-permute-done = f32[2,10,128]{2,0,1:T(2,128)S(1)} collective-permute-done((f32[2,10,128]{2,0,1:T(2,128)S(1)}, f32[2,10,128]{2,0,1:T(2,128)S(1)}, u32[]{:S(2)}, u32[]{:S(2)}) %collective-permute-start) | collective-permute-done | bytes 10272 | tf_op jit(solution)/shard_map/ppermute | solution.py:19
  95.2 3.5 %collective-permute-start.2 = (f32[2,4,128]{2,1,0:T(4,128)S(1)}, f32[2,4,128]{2,1,0:T(4,128)S(1)}, u32[]{:S(2)}, u32[]{:S(2)}) collective-permute-start(f32[2,4,128]{2,1,0:T(4,128)S(1)} %get-tuple-element.9), channel_id=1, source_target_pairs={{0,1},{1,2},{2,3},{3,4},{4,5},{5,6},{6,7},{7,8},{8,9},{9,10},{10,1... | collective-permute-start | bytes 12296 | tf_op jit(solution)/shard_map/ppermute | solution.py:19
  98.8 2.3 %collective-permute-start.3 = (f32[2,4,128]{2,1,0:T(4,128)S(1)}, f32[2,4,128]{2,1,0:T(4,128)S(1)}, u32[]{:S(2)}, u32[]{:S(2)}) collective-permute-start(f32[2,4,128]{2,1,0:T(4,128)S(1)} %get-tuple-element.8), channel_id=1, source_target_pairs={{1,0},{2,1},{3,2},{4,3},{5,4},{6,5},{7,6},{8,7},{9,8},{10,9},{11,1... | collective-permute-start | bytes 12296 | tf_op jit(solution)/shard_map/ppermute | solution.py:19
  101.2 0.0 collective-permute-done.2
  101.2 5.3 %collective-permute-done.3 = f32[2,4,128]{2,1,0:T(4,128)S(1)} collective-permute-done((f32[2,4,128]{2,1,0:T(4,128)S(1)}, f32[2,4,128]{2,1,0:T(4,128)S(1)}, u32[]{:S(2)}, u32[]{:S(2)}) %collective-permute-start.3) | collective-permute-done | bytes 4128 | tf_op jit(solution)/shard_map/ppermute | solution.py:19
  106.5 0.6 slice_bitcast_fusion
  (10 shorter events, 0.1 us)
Async XLA Ops:
  87.1 5.1 %collective-permute-start.1 = (f32[2,10,128]{2,0,1:T(2,128)S(1)}, f32[2,10,128]{2,0,1:T(2,128)S(1)}, u32[]{:S(2)}, u32[]{:S(2)}) collective-permute-start(f32[2,10,128]{2,0,1:T(2,128)S(1)} %bitcast.39), channel_id=1, source_target_pairs={{16,0},{32,16},{48,32},{64,48},{80,64},{96,80},{112,96},{17,1},{33... | collective-permute-start | bytes 30728 | tf_op jit(solution)/shard_map/ppermute | solution.py:19
  90.2 5.0 %collective-permute-start = (f32[2,10,128]{2,0,1:T(2,128)S(1)}, f32[2,10,128]{2,0,1:T(2,128)S(1)}, u32[]{:S(2)}, u32[]{:S(2)}) collective-permute-start(f32[2,10,128]{2,0,1:T(2,128)S(1)} %bitcast.40), channel_id=1, source_target_pairs={{0,16},{16,32},{32,48},{48,64},{64,80},{80,96},{96,112},{1,17},{17... | collective-permute-start | bytes 30728 | tf_op jit(solution)/shard_map/ppermute | solution.py:19
  95.2 5.9 %collective-permute-start.2 = (f32[2,4,128]{2,1,0:T(4,128)S(1)}, f32[2,4,128]{2,1,0:T(4,128)S(1)}, u32[]{:S(2)}, u32[]{:S(2)}) collective-permute-start(f32[2,4,128]{2,1,0:T(4,128)S(1)} %get-tuple-element.9), channel_id=1, source_target_pairs={{0,1},{1,2},{2,3},{3,4},{4,5},{5,6},{6,7},{7,8},{8,9},{9,10},{10,1... | collective-permute-start | bytes 12296 | tf_op jit(solution)/shard_map/ppermute | solution.py:19
  98.8 7.6 %collective-permute-start.3 = (f32[2,4,128]{2,1,0:T(4,128)S(1)}, f32[2,4,128]{2,1,0:T(4,128)S(1)}, u32[]{:S(2)}, u32[]{:S(2)}) collective-permute-start(f32[2,4,128]{2,1,0:T(4,128)S(1)} %get-tuple-element.8), channel_id=1, source_target_pairs={{1,0},{2,1},{3,2},{4,3},{5,4},{6,5},{7,6},{8,7},{9,8},{10,9},{11,1... | collective-permute-start | bytes 12296 | tf_op jit(solution)/shard_map/ppermute | solution.py:19

commit v2 on v1

v2 whole, which is shorter than its diff:
```python
import jax
import jax.numpy as jnp
from jax import lax
from jax.experimental import pallas as pl
from jax.experimental.pallas import tpu as pltpu
from jax.sharding import PartitionSpec as P

BX = 4
BY = 8
BZ = 128
CAP = 2
ROWS = 64
GROUP = 8
LANES = 128


def passed_along(value, axis, steps):
    count = lax.axis_size(axis)
    first, last = (max(0, -steps), min(count, count - steps))
    return lax.ppermute(value, axis, [(source, source + steps) for source in range(first, last)])


def dispatch_kernel(ids_ref, count_ref, offset_ref, frac_ref, normal_ref, weight_ref, out_ref, seen_ref):
    slots = out_ref.shape[0]

    def clear(i, _):
        out_ref[pl.ds(i * 8, 8)] = jnp.zeros((8,) + out_ref.shape[1:], jnp.float32)
        return 0

    lax.fori_loop(0, slots // 8, clear, 0)

    def reset(i, _):
        seen_ref[i] = 0
        return 0

    lax.fori_loop(0, seen_ref.shape[0], reset, 0)

    def place(t, _):
        brick = ids_ref[t]
        rank = seen_ref[brick]
        seen_ref[brick] = rank + 1
        slot = brick * CAP + jnp.minimum(rank, CAP - 1)
        here = pl.ds(t, 1)
        rows = [frac_ref[k, here, :] for k in range(3)] + [offset_ref[here, :].astype(jnp.float32)]
        rows += [normal_ref[k, here, :] for k in range(3)] + [weight_ref[here, :]]
        for half in range(out_ref.shape[1] // 8):
            for k, row in enumerate(rows):
                out_ref[slot, 8 * half + k : 8 * half + k + 1, :] = row[:, LANES * half : LANES * half + LANES]
        return 0

    lax.fori_loop(0, jnp.minimum(count_ref[0], ids_ref.shape[0]), place, 0)


def dispatch(ids, count, offset, frac, normal, weight, bricks):
    smem = pl.BlockSpec(memory_space=pltpu.SMEM)
    vmem = pl.BlockSpec(memory_space=pltpu.VMEM)
    return pl.pallas_call(
        dispatch_kernel,
        out_shape=jax.ShapeDtypeStruct((bricks * CAP, 8 * offset.shape[1] // LANES, LANES), jnp.float32),
        in_specs=[smem, smem, vmem, vmem, vmem, vmem],
        out_specs=vmem,
        scratch_shapes=[pltpu.SMEM((bricks,), jnp.int32)],
        name="dispatch",
    )(ids, count, offset, frac, normal, weight)


def bspline(t):
    outer = jnp.maximum(1.5 - jnp.abs(t), 0.0)
    inner = jnp.maximum(outer - 1.0, 0.0)
    value = outer * outer - 3.0 * (inner * inner)
    slope = jnp.minimum(jnp.maximum(t + t, -outer), outer)
    return value, slope


def prepare(inbox_ref, group, half, prep_ref):
    per_tile = 8 * prep_ref.shape[0]

    def channel(c):
        return inbox_ref[pl.ds(group * (per_tile * GROUP) + 8 * half + c, GROUP, stride=per_tile), :]

    offset = channel(3).astype(jnp.int32)
    at_x = lax.shift_right_logical(offset, 10).astype(jnp.float32) + channel(0)
    at_y = (lax.shift_right_logical(offset, 7) & 7).astype(jnp.float32) + channel(1)
    rows = [at_x, at_y]
    for s in (BY, BY + 1):
        rows.extend(bspline((s - 0.5) - at_y))
    fz = channel(2)
    rows.extend([0.5 * (1.0 - fz) * (1.0 - fz), 0.75 - (fz - 0.5) * (fz - 0.5), 0.5 * fz * fz])
    rows.extend([fz - 1.0, 1.0 - 2.0 * fz, fz])
    cell_z = offset & 127
    for k in (-1, 0, 1):
        rows.append(((cell_z + k) & 15).astype(jnp.float32))
    for k in (-1, 0, 1):
        rows.append(lax.shift_right_arithmetic(cell_z + k, 4).astype(jnp.float32))
    rows.extend([channel(4), channel(5), channel(6), channel(7)])
    for i, row in enumerate(rows):
        prep_ref[half, i] = row


def build(prep_ref, half, tile, x_ref):
    def row(i):
        return jnp.broadcast_to(prep_ref[half, i, tile : tile + 1, :], (8, LANES))

    def paired(i):
        v = row(i)
        return jnp.concatenate([v, v], axis=0).astype(jnp.bfloat16)

    sub = lax.broadcasted_iota(jnp.int32, (8, LANES), 0).astype(jnp.float32) - 0.5
    x_value, x_slope = bspline(sub - row(0))
    y_value, y_slope = bspline(sub - row(1))
    factors = [row(18) * x_slope, row(19) * x_value, row(20) * x_value, row(21) * x_value]
    for i, v in enumerate(factors):
        x_ref[i] = v

    def planes(one, two, three, screen, yv, ys):
        return [one * yv + two * ys, three * yv, screen * yv]

    left = [[], [], []]
    for pair in range(4):
        blocks = []
        for p in (2 * pair, 2 * pair + 1):
            if p < BX + 2:
                wide = [jnp.broadcast_to(x_ref[i, p : p + 1, :], (8, LANES)) for i in range(4)]
                blocks.append(planes(*wide, y_value, y_slope))
            else:
                s = p - (BX + 2)
                blocks.append(planes(*factors, row(2 + 2 * s), row(3 + 2 * s)))
        for k in range(3):
            left[k].append(jnp.concatenate([blocks[0][k], blocks[1][k]], axis=0).astype(jnp.bfloat16))

    zero = jnp.zeros((16, LANES), jnp.bfloat16)
    depth = lax.broadcasted_iota(jnp.int32, (16, LANES), 0).astype(jnp.float32).astype(jnp.bfloat16)
    hits = [depth == paired(12 + k) for k in range(3)]

    def pick(first, default):
        return jnp.where(hits[0], paired(first), jnp.where(hits[1], paired(first + 1), default))

    value = pick(6, jnp.where(hits[2], paired(8), zero))
    slope = pick(9, jnp.where(hits[2], paired(11), zero))
    home = pick(15, paired(17))
    right = [[], []]
    for block in range(BZ // 16):
        inside = home == jnp.full((16, LANES), block, jnp.bfloat16)
        right[0].append(jnp.where(inside, value, zero))
        right[1].append(jnp.where(inside, slope, zero))
    return jnp.concatenate(sum(left, []), axis=0), jnp.concatenate(sum(right, []), axis=0)


def splat_kernel(inbox_ref, field_ref, up_ref, down_ref, acc_ref, prep_ref, x_ref):
    halves = prep_ref.shape[0]
    slots = inbox_ref.shape[0] // (8 * halves)
    acc_ref[...] = jnp.zeros_like(acc_ref)

    def body(group, _):
        for half in range(halves):
            prepare(inbox_ref, group, half, prep_ref)
        acc = acc_ref[...]
        for tile in range(GROUP):
            sides = [build(prep_ref, half, tile, x_ref.at[(tile * halves + half) % 4]) for half in range(halves)]
            acc = acc + lax.dot_general(
                jnp.concatenate([a for a, _ in sides], axis=1),
                jnp.concatenate([z for _, z in sides], axis=1),
                (((1,), (1,)), ((), ())),
                preferred_element_type=jnp.float32,
            )
        acc_ref[...] = acc
        return 0

    lax.fori_loop(0, slots // GROUP, body, 0)
    field_ref[0] = 0.5 * acc_ref[0:ROWS, 0:BZ] + 0.25 * acc_ref[ROWS : 2 * ROWS, BZ : 2 * BZ]
    field_ref[1] = 0.25 * acc_ref[2 * ROWS : 3 * ROWS, 0:BZ]
    tail = jnp.zeros((4, BZ), jnp.float32)
    for ref, r in ((up_ref, BX + 1), (down_ref, 0)):
        for c in range(2):
            ref[8 * c : 8 * c + 8, :] = field_ref[c, 8 * r : 8 * r + 8, :]
            for s in range(2):
                ref[16 + 2 * c + s : 17 + 2 * c + s, :] = field_ref[c, 48 + 8 * s + r : 49 + 8 * s + r, :]
        ref[20:24, :] = tail


def splat(inbox, halves):
    vmem = pl.BlockSpec(memory_space=pltpu.VMEM)
    return pl.pallas_call(
        splat_kernel,
        out_shape=(
            jax.ShapeDtypeStruct((2, ROWS, BZ), jnp.float32),
            jax.ShapeDtypeStruct((24, BZ), jnp.float32),
            jax.ShapeDtypeStruct((24, BZ), jnp.float32),
        ),
        in_specs=[vmem],
        out_specs=(vmem, vmem, vmem),
        scratch_shapes=[
            pltpu.VMEM((3 * ROWS, 2 * BZ), jnp.float32),
            pltpu.VMEM((halves, 22, GROUP, LANES), jnp.float32),
            pltpu.VMEM((4, 4, 8, LANES), jnp.float32),
        ],
        name="splat",
    )(inbox)


def face_rows(face):
    ends = face[16:20].reshape(2, 2, BZ)
    return jnp.concatenate([face[0:16].reshape(2, BY, BZ), ends], axis=1)


def shards(brick_ids, voxel_offset, fractions, normals, point_weight, tile_count):
    bricks = lax.axis_size("gx") * lax.axis_size("yz")
    outbox = dispatch(
        brick_ids[:, 0],
        tile_count,
        voxel_offset,
        jnp.transpose(fractions, (1, 0, 2)),
        jnp.transpose(normals, (1, 0, 2)),
        point_weight,
        bricks,
    )
    inbox = lax.all_to_all(outbox, ("gx", "yz"), split_axis=0, concat_axis=0, tiled=True)
    field, up, down = splat(inbox.reshape(-1, LANES), inbox.shape[1] // 8)
    from_below = passed_along(up, "gx", 1)
    from_above = passed_along(down, "gx", -1)
    main = field[:, 8 : 8 * (BX + 1)].reshape(2, BX, BY, BZ)
    ends = field[:, 48:64].reshape(2, 2, 8, BZ)[:, :, 1 : BX + 1]
    inner = jnp.concatenate([main, jnp.transpose(ends, (0, 2, 1, 3))], axis=2)
    inner = jnp.concatenate(
        [
            inner[:, :1] + face_rows(from_below)[:, None],
            inner[:, 1 : BX - 1],
            inner[:, BX - 1 :] + face_rows(from_above)[:, None],
        ],
        axis=1,
    )
    from_left = passed_along(inner[:, :, BY + 1].reshape(2 * BX, BZ), "yz", 1).reshape(2, BX, 1, BZ)
    from_right = passed_along(inner[:, :, 0].reshape(2 * BX, BZ), "yz", -1).reshape(2, BX, 1, BZ)
    result = jnp.concatenate(
        [inner[:, :, 1:2] + from_left, inner[:, :, 2:BY], inner[:, :, BY : BY + 1] + from_right], axis=2
    )
    return (result[0], result[1])


def solution(mesh):
    return jax.shard_map(
        shards,
        mesh=mesh,
        in_specs=(
            P(("gx", "yz"), None),
            P(("gx", "yz"), None),
            P(("gx", "yz"), None, None),
            P(("gx", "yz"), None, None),
            P(("gx", "yz"), None),
            P(("gx", "yz")),
        ),
        out_specs=(P("gx", "yz", None), P("gx", "yz", None)),
        check_vma=False,
    )
```

time: 108 us -> 90 us (0.83)
  the two profiles are of different devices: /device:TPU:38 before, /device:TPU:40 now
where the time goes in v2:
time: 90 us; the launch traced here: 89.4 us
  blocking collectives  39.2 us (44%)
  Pallas kernels  26.5 us (29%)
  starting transfers between devices  10.4 us (12%)
  waiting for transfers between devices  9.74 us (11%)
  local copies, waits for them, and re-layouts  2.12 us (2%)
  between operations  1.38 us (2%)
    all_to_all x1, blocking collectives, shards(): lax.all_to_all(outbox, ('gx', 'yz'), split_axis=0, concat_axis=0, tiled=T...  39.2 us
    pallas_call x1, Pallas kernels, splat(): pl.pallas_call(splat_kernel, out_shape=(jax.ShapeDtypeStruct((2, ROWS, BZ...  21.7 us
    ppermute x4, starting transfers between devices, passed_along(): lax.ppermute(value, axis, [(source, source + steps) for source in range(f...  10.4 us
    ppermute x4, waiting for transfers between devices, passed_along(): lax.ppermute(value, axis, [(source, source + steps) for source in range(f...  9.74 us
    pallas_call x1, Pallas kernels, dispatch(): pl.pallas_call(dispatch_kernel, out_shape=jax.ShapeDtypeStruct((bricks *...  4.83 us
  transfers between devices with their start and end apart: 4, of which 3 were waited for; matrix products, arithmetic and copies ran while one was open for 0% of the time, Pallas kernels for 0%

profile of v2, /device:TPU:40, one launch (start us, length us, event | category | flops | bytes accessed | tf_op | source)
XLA Modules:
  0.0 89.4 jit_solution(5013609841829171131)
XLA Ops:
  1.3 4.8 %dispatch.1 = f32[256,16,128]{2,1,0:T(8,128)} custom-call(s32[128]{0:T(128)} %bitcast.44, s32[1]{0:T(128)S(6)} %copy.12.count_ref, s32[128,256]{1,0:T(8,128)} %offset_ref.1, f32[3,128,256]{2,1,0:T(8,128)} %bitcast.34, f32[3,128,256]{2,1,0:T(8,128)} %bitcast.35, f32[128,256]{1,0:T(8,128)} %weight_ref.1), custom_call_target="tpu_custom_call" | custom-call | tf_op jit(solution)/shard_map/dispatch/pallas_call | solution.py:57
  6.1 39.2 %all_to_all.5 = f32[256,16,128]{2,1,0:T(8,128)} all-to-all(f32[256,16,128]{2,1,0:T(8,128)} %dispatch.1), channel_id=1, replica_groups=mesh['gx'=8,'yz'=16] {'gx','yz'}, dimensions={0} | all-to-all | bytes 4194304 | tf_op jit(solution)/shard_map/all_to_all | solution.py:217
  45.3 21.7 %splat.1 = (f32[2,64,128]{2,1,0:T(8,128)}, f32[24,128]{1,0:T(8,128)}, f32[24,128]{1,0:T(8,128)}) custom-call(f32[4096,128]{1,0:T(8,128)} %bitcast.33), custom_call_target="tpu_custom_call" | custom-call | tf_op jit(solution)/shard_map/splat/pallas_call | solution.py:183
  67.0 0.7 slice_bitcast_fusion.3
  67.7 0.8 slice_bitcast_fusion
  68.5 1.9 %collective-permute-start = (f32[24,128]{1,0:T(8,128)}, f32[24,128]{1,0:T(8,128)S(1)}, u32[]{:S(2)}, u32[]{:S(2)}) collective-permute-start(f32[24,128]{1,0:T(8,128)} %get-tuple-element.6), channel_id=1, source_target_pairs={{0,16},{16,32},{32,48},{48,64},{64,80},{80,96},{96,112},{1,17},{17... | collective-permute-start | bytes 36872 | tf_op jit(solution)/shard_map/ppermute | solution.py:20
  70.4 3.6 %collective-permute-start.1 = (f32[24,128]{1,0:T(8,128)}, f32[24,128]{1,0:T(8,128)S(1)}, u32[]{:S(2)}, u32[]{:S(2)}) collective-permute-start(f32[24,128]{1,0:T(8,128)} %get-tuple-element.7), channel_id=1, source_target_pairs={{16,0},{32,16},{48,32},{64,48},{80,64},{96,80},{112,96},{17,1},{33... | collective-permute-start | bytes 36872 | tf_op jit(solution)/shard_map/ppermute | solution.py:20
  74.1 0.0 collective-permute-done
  74.1 1.5 %collective-permute-done.1 = f32[24,128]{1,0:T(8,128)S(1)} collective-permute-done((f32[24,128]{1,0:T(8,128)}, f32[24,128]{1,0:T(8,128)S(1)}, u32[]{:S(2)}, u32[]{:S(2)}) %collective-permute-start.1) | collective-permute-done | bytes 12320 | tf_op jit(solution)/shard_map/ppermute | solution.py:20
  75.7 2.8 %collective-permute-start.2 = (f32[8,128]{1,0:T(8,128)S(1)}, f32[8,128]{1,0:T(8,128)S(1)}, u32[]{:S(2)}, u32[]{:S(2)}) collective-permute-start(f32[8,128]{1,0:T(8,128)S(1)} %bitcast.43), channel_id=1, source_target_pairs={{0,1},{1,2},{2,3},{3,4},{4,5},{5,6},{6,7},{7,8},{8,9},{9,10},{10,1... | collective-permute-start | bytes 12296 | tf_op jit(solution)/shard_map/ppermute | solution.py:20
  78.5 4.8 %collective-permute-done.2 = f32[8,128]{1,0:T(8,128)S(1)} collective-permute-done((f32[8,128]{1,0:T(8,128)S(1)}, f32[8,128]{1,0:T(8,128)S(1)}, u32[]{:S(2)}, u32[]{:S(2)}) %collective-permute-start.2) | collective-permute-done | bytes 4128 | tf_op jit(solution)/shard_map/ppermute | solution.py:20
  83.3 2.0 %collective-permute-start.3 = (f32[8,128]{1,0:T(8,128)S(1)}, f32[8,128]{1,0:T(8,128)S(1)}, u32[]{:S(2)}, u32[]{:S(2)}) collective-permute-start(f32[8,128]{1,0:T(8,128)S(1)} %bitcast.41), channel_id=1, source_target_pairs={{1,0},{2,1},{3,2},{4,3},{5,4},{6,5},{7,6},{8,7},{9,8},{10,9},{11,1... | collective-permute-start | bytes 12296 | tf_op jit(solution)/shard_map/ppermute | solution.py:20
  85.4 3.4 %collective-permute-done.3 = f32[8,128]{1,0:T(8,128)S(1)} collective-permute-done((f32[8,128]{1,0:T(8,128)S(1)}, f32[8,128]{1,0:T(8,128)S(1)}, u32[]{:S(2)}, u32[]{:S(2)}) %collective-permute-start.3) | collective-permute-done | bytes 4128 | tf_op jit(solution)/shard_map/ppermute | solution.py:20
  88.8 0.6 slice_bitcast_fusion.1
  (14 shorter events, 0.1 us)
Async XLA Ops:
  68.5 5.6 %collective-permute-start = (f32[24,128]{1,0:T(8,128)}, f32[24,128]{1,0:T(8,128)S(1)}, u32[]{:S(2)}, u32[]{:S(2)}) collective-permute-start(f32[24,128]{1,0:T(8,128)} %get-tuple-element.6), channel_id=1, source_target_pairs={{0,16},{16,32},{32,48},{48,64},{64,80},{80,96},{96,112},{1,17},{17... | collective-permute-start | bytes 36872 | tf_op jit(solution)/shard_map/ppermute | solution.py:20
  70.4 5.2 %collective-permute-start.1 = (f32[24,128]{1,0:T(8,128)}, f32[24,128]{1,0:T(8,128)S(1)}, u32[]{:S(2)}, u32[]{:S(2)}) collective-permute-start(f32[24,128]{1,0:T(8,128)} %get-tuple-element.7), channel_id=1, source_target_pairs={{16,0},{32,16},{48,32},{64,48},{80,64},{96,80},{112,96},{17,1},{33... | collective-permute-start | bytes 36872 | tf_op jit(solution)/shard_map/ppermute | solution.py:20
  75.7 7.6 %collective-permute-start.2 = (f32[8,128]{1,0:T(8,128)S(1)}, f32[8,128]{1,0:T(8,128)S(1)}, u32[]{:S(2)}, u32[]{:S(2)}) collective-permute-start(f32[8,128]{1,0:T(8,128)S(1)} %bitcast.43), channel_id=1, source_target_pairs={{0,1},{1,2},{2,3},{3,4},{4,5},{5,6},{6,7},{7,8},{8,9},{9,10},{10,1... | collective-permute-start | bytes 12296 | tf_op jit(solution)/shard_map/ppermute | solution.py:20
  83.3 5.5 %collective-permute-start.3 = (f32[8,128]{1,0:T(8,128)S(1)}, f32[8,128]{1,0:T(8,128)S(1)}, u32[]{:S(2)}, u32[]{:S(2)}) collective-permute-start(f32[8,128]{1,0:T(8,128)S(1)} %bitcast.41), channel_id=1, source_target_pairs={{1,0},{2,1},{3,2},{4,3},{5,4},{6,5},{7,6},{8,7},{9,8},{10,9},{11,1... | collective-permute-start | bytes 12296 | tf_op jit(solution)/shard_map/ppermute | solution.py:20

commit v3 on v2

v3 whole, which is shorter than its diff:
```python
import jax
import jax.numpy as jnp
from jax import lax
from jax.experimental import pallas as pl
from jax.experimental.pallas import tpu as pltpu
from jax.sharding import PartitionSpec as P

BX = 4
BY = 8
BZ = 128
CAP = 2
LANES = 128
GROUP = 8
UNROLL = 8
PLANES = (BX + 2) * BY
ENDS = 16
ROWS = PLANES + ENDS
ROW_X = 0
ROW_Z = 4 * (BX + 2)
ROW_COUNT = ROW_Z + 8
SIDES = 8


def passed_along(value, axis, steps):
    count = lax.axis_size(axis)
    return lax.ppermute(value, axis, [(source, (source + steps) % count) for source in range(count)])


def dispatch_kernel(ids_ref, count_ref, offset_ref, frac_ref, normal_ref, weight_ref, out_ref, seen_ref):
    slots = out_ref.shape[0]

    def clear(i, _):
        out_ref[pl.ds(i * 8, 8)] = jnp.zeros((8,) + out_ref.shape[1:], jnp.float32)
        return 0

    lax.fori_loop(0, slots // 8, clear, 0)

    def reset(i, _):
        seen_ref[i] = 0
        return 0

    lax.fori_loop(0, seen_ref.shape[0], reset, 0)

    def place(t, _):
        brick = ids_ref[t]
        rank = seen_ref[brick]
        seen_ref[brick] = rank + 1
        slot = brick * CAP + jnp.minimum(rank, CAP - 1)
        here = pl.ds(t, 1)
        rows = [frac_ref[k, here, :] for k in range(3)] + [offset_ref[here, :].astype(jnp.float32)]
        rows += [normal_ref[k, here, :] for k in range(3)] + [weight_ref[here, :]]
        for half in range(out_ref.shape[1] // 8):
            for k, row in enumerate(rows):
                out_ref[slot, 8 * half + k : 8 * half + k + 1, :] = row[:, LANES * half : LANES * half + LANES]
        return 0

    lax.fori_loop(0, jnp.minimum(count_ref[0], ids_ref.shape[0]), place, 0)


def dispatch(ids, count, offset, frac, normal, weight, bricks):
    smem = pl.BlockSpec(memory_space=pltpu.SMEM)
    vmem = pl.BlockSpec(memory_space=pltpu.VMEM)
    return pl.pallas_call(
        dispatch_kernel,
        out_shape=jax.ShapeDtypeStruct((bricks * CAP, 8 * offset.shape[1] // LANES, LANES), jnp.float32),
        in_specs=[smem, smem, vmem, vmem, vmem, vmem],
        out_specs=vmem,
        scratch_shapes=[pltpu.SMEM((bricks,), jnp.int32)],
        name="dispatch",
    )(ids, count, offset, frac, normal, weight)


def spline(f):
    return (
        [0.5 * (1.0 - f) * (1.0 - f), 0.75 - (f - 0.5) * (f - 0.5), 0.5 * f * f],
        [f - 1.0, 1.0 - 2.0 * f, f],
    )


def spread(cell, cells, pieces):
    here = [cell == c for c in range(cells)]
    out = []
    for target in range(cells + 2):
        value = None
        for i in range(3):
            c = target - i
            if 0 <= c < cells:
                value = jnp.where(here[c], pieces[i], 0.0 if value is None else value)
        out.append(value)
    return out


def prepare(inbox_ref, first, row_ref, side_ref):
    def channel(c):
        return inbox_ref[pl.ds(first * 8 + c, GROUP, stride=8), :]

    offset = channel(3).astype(jnp.int32)
    weights, slopes = spline(channel(0))
    cell = lax.shift_right_logical(offset, 10)
    x_value, x_slope = spread(cell, BX, weights), spread(cell, BX, slopes)
    weights, slopes = spline(channel(1))
    cell = lax.shift_right_logical(offset, 7) & 7
    y_value, y_slope = spread(cell, BY, weights), spread(cell, BY, slopes)
    nx, ny, nz, weight = [channel(c) for c in (4, 5, 6, 7)]
    for r in range(BX + 2):
        parts = (nx * x_slope[r], ny * x_value[r], nz * x_value[r], weight * x_value[r])
        for i, part in enumerate(parts):
            row_ref[ROW_X + 4 * r + i] = part
        for e in range(2):
            yv, ys = y_value[BY + e], y_slope[BY + e]
            ends = (parts[0] * yv + parts[1] * ys, parts[2] * yv, parts[3] * yv)
            for k in range(3):
                side_ref[2 * k + e, GROUP * r : GROUP * r + GROUP, :] = ends[k]
    for s in range(BY):
        side_ref[6, GROUP * s : GROUP * s + GROUP, :] = y_value[s]
        side_ref[7, GROUP * s : GROUP * s + GROUP, :] = y_slope[s]
    weights, slopes = spline(channel(2))
    cell = offset & 127
    rows = weights + slopes + [(cell & 15).astype(jnp.float32), lax.shift_right_logical(cell, 4).astype(jnp.float32)]
    for i, row in enumerate(rows):
        row_ref[ROW_Z + i] = row


def build(row_ref, side_ref, unit):
    def row(i):
        return jnp.broadcast_to(row_ref[i, unit : unit + 1, :], (8, LANES))

    def paired(i):
        v = row(i)
        return jnp.concatenate([v, v], axis=0).astype(jnp.bfloat16)

    def side(i):
        return side_ref[i, pl.ds(unit, 8, stride=GROUP), :]

    y_value, y_slope = side(6), side(7)
    left = [[], [], []]
    for pair in range((BX + 2) // 2):
        blocks = []
        for r in (2 * pair, 2 * pair + 1):
            one, two, three, screen = [row(ROW_X + 4 * r + i) for i in range(4)]
            blocks.append((one * y_value + two * y_slope, three * y_value, screen * y_value))
        for k in range(3):
            left[k].append(jnp.concatenate([blocks[0][k], blocks[1][k]], axis=0).astype(jnp.bfloat16))
    for k in range(3):
        left[k].append(jnp.concatenate([side(2 * k), side(2 * k + 1)], axis=0).astype(jnp.bfloat16))

    depth = lax.broadcasted_iota(jnp.int32, (16, LANES), 0)
    zero = jnp.zeros((16, LANES), jnp.bfloat16)

    def constant(v):
        return v.astype(jnp.float32).astype(jnp.bfloat16)

    low, block_of = paired(ROW_Z + 6), paired(ROW_Z + 7)
    w = [paired(ROW_Z + i) for i in range(6)]
    below = constant((depth + 1) & 15) == low
    value, slope = jnp.where(below, w[0], zero), jnp.where(below, w[3], zero)
    carry = jnp.where(below, constant(jnp.where(depth == 15, -1, 0)), zero)
    same = constant(depth) == low
    value, slope = jnp.where(same, w[1], value), jnp.where(same, w[4], slope)
    above = constant((depth + 15) & 15) == low
    value, slope = jnp.where(above, w[2], value), jnp.where(above, w[5], slope)
    home = block_of + jnp.where(above, constant(jnp.where(depth == 0, 1, 0)), carry)
    right = [[], []]
    for block in range(BZ // 16):
        inside = home == jnp.full((16, LANES), block, jnp.bfloat16)
        right[0].append(jnp.where(inside, value, zero))
        right[1].append(jnp.where(inside, slope, zero))
    return jnp.concatenate(sum(left, []), axis=0), jnp.concatenate(sum(right, []), axis=0)


def splat_kernel(inbox_ref, field_ref, up_ref, down_ref, right_ref, left_ref, acc_ref, row_ref, side_ref):
    batch = GROUP * UNROLL
    steps = inbox_ref.shape[0] // (8 * batch)

    acc_ref[...] = jnp.zeros_like(acc_ref)

    def body(i, _):
        for u in range(UNROLL):
            prepare(inbox_ref, i * batch + u * GROUP, row_ref.at[u], side_ref.at[u])
        acc = acc_ref[...]
        for pair in range(batch // 2):
            sides = [build(row_ref.at[k // GROUP], side_ref.at[k // GROUP], k % GROUP) for k in (2 * pair, 2 * pair + 1)]
            acc = acc + lax.dot_general(
                jnp.concatenate([a for a, _ in sides], axis=1),
                jnp.concatenate([z for _, z in sides], axis=1),
                (((1,), (1,)), ((), ())),
                preferred_element_type=jnp.float32,
            )
        acc_ref[...] = acc
        return 0

    lax.fori_loop(0, steps, body, 0)
    for k in range(2):
        first = 2 * ROWS * k
        if k == 0:
            acc_ref[0:ROWS, 0:BZ] = acc_ref[0:ROWS, 0:BZ] + acc_ref[ROWS : 2 * ROWS, BZ : 2 * BZ]

        def rows(at, count, first=first):
            return acc_ref[first + at : first + at + count, 0:BZ]

        for r in range(BX):
            field_ref[k, r, 0 : BY - 1, :] = rows(BY * (r + 1) + 1, BY - 1)
            field_ref[k, r, BY - 1 : BY, :] = rows(PLANES + r + 1, 1)
            left_ref[BX * k + r : BX * k + r + 1, :] = rows(BY * (r + 1), 1)
        right_ref[BX * k : BX * k + BX, :] = rows(PLANES + 9, BX)
        for ref, r in ((up_ref, BX + 1), (down_ref, 0)):
            ref[BY * k : BY * k + BY - 1, :] = rows(BY * r + 1, BY - 1)
            ref[BY * k + BY - 1 : BY * k + BY, :] = rows(PLANES + r, 1)
            ref[16 + k : 17 + k, :] = rows(BY * r, 1)
            ref[18 + k : 19 + k, :] = rows(PLANES + 8 + r, 1)
    for ref in (up_ref, down_ref):
        ref[20:24, :] = jnp.zeros((4, BZ), jnp.float32)


def splat(inbox):
    vmem = pl.BlockSpec(memory_space=pltpu.VMEM)
    shapes = ((2, BX, BY, BZ), (24, BZ), (24, BZ), (2 * BX, BZ), (2 * BX, BZ))
    return pl.pallas_call(
        splat_kernel,
        out_shape=tuple(jax.ShapeDtypeStruct(shape, jnp.float32) for shape in shapes),
        in_specs=[vmem],
        out_specs=(vmem,) * len(shapes),
        scratch_shapes=[
            pltpu.VMEM((3 * ROWS, 2 * BZ), jnp.float32),
            pltpu.VMEM((UNROLL, ROW_COUNT, GROUP, LANES), jnp.float32),
            pltpu.VMEM((UNROLL, SIDES, 8 * GROUP, LANES), jnp.float32),
        ],
        compiler_params=pltpu.CompilerParams(vmem_limit_bytes=16 * 1024 * 1024),
        name="splat",
    )(inbox)


def join_kernel(edge_ref, below_ref, above_ref, right_ref, left_ref, right_out, left_out):
    below = jnp.where(edge_ref[0] == 0, 0.0, below_ref[16:24, :])
    above = jnp.where(edge_ref[1] == 0, 0.0, above_ref[16:24, :])
    right_out[...] = right_ref[...]
    left_out[...] = left_ref[...]
    for k in range(2):
        for out, at in ((left_out, k), (right_out, 2 + k)):
            first, last = BX * k, BX * k + BX - 1
            out[first : first + 1, :] = out[first : first + 1, :] + below[at : at + 1]
            out[last : last + 1, :] = out[last : last + 1, :] + above[at : at + 1]


def join(edges, below, above, right, left):
    smem = pl.BlockSpec(memory_space=pltpu.SMEM)
    vmem = pl.BlockSpec(memory_space=pltpu.VMEM)
    shape = jax.ShapeDtypeStruct(right.shape, jnp.float32)
    return pl.pallas_call(
        join_kernel,
        out_shape=(shape, shape),
        in_specs=[smem] + [vmem] * 4,
        out_specs=(vmem, vmem),
        compiler_params=pltpu.CompilerParams(vmem_limit_bytes=4 * 1024 * 1024),
        name="join",
    )(edges, below, above, right, left)


def finish_kernel(edge_ref, field_ref, below_ref, above_ref, before_ref, after_ref, rhs_ref, screen_ref):
    for k, ref in enumerate((rhs_ref, screen_ref)):
        for r in range(BX):
            plane = field_ref[k, r]
            if r == 0:
                plane = plane + jnp.where(edge_ref[0] == 0, 0.0, below_ref[BY * k : BY * k + BY, :])
            if r == BX - 1:
                plane = plane + jnp.where(edge_ref[1] == 0, 0.0, above_ref[BY * k : BY * k + BY, :])
            ref[r] = plane
            at = BX * k + r
            before = jnp.where(edge_ref[2] == 0, 0.0, before_ref[at : at + 1, :])
            after = jnp.where(edge_ref[3] == 0, 0.0, after_ref[at : at + 1, :])
            ref[r, 0:1, :] = ref[r, 0:1, :] + before
            ref[r, BY - 1 : BY, :] = ref[r, BY - 1 : BY, :] + after


def finish(edges, field, below, above, before, after):
    smem = pl.BlockSpec(memory_space=pltpu.SMEM)
    vmem = pl.BlockSpec(memory_space=pltpu.VMEM)
    shape = jax.ShapeDtypeStruct((BX, BY, BZ), jnp.float32)
    return pl.pallas_call(
        finish_kernel,
        out_shape=(shape, shape),
        in_specs=[smem] + [vmem] * 5,
        out_specs=(vmem, vmem),
        compiler_params=pltpu.CompilerParams(vmem_limit_bytes=4 * 1024 * 1024),
        name="finish",
    )(edges, field, below, above, before, after)


def shards(brick_ids, voxel_offset, fractions, normals, point_weight, tile_count):
    slabs, columns = lax.axis_size("gx"), lax.axis_size("yz")
    outbox = dispatch(
        brick_ids[:, 0],
        tile_count,
        voxel_offset,
        jnp.transpose(fractions, (1, 0, 2)),
        jnp.transpose(normals, (1, 0, 2)),
        point_weight,
        slabs * columns,
    )
    inbox = lax.all_to_all(outbox, ("gx", "yz"), split_axis=0, concat_axis=0, tiled=True)
    slab, column = lax.axis_index("gx"), lax.axis_index("yz")
    edges = jnp.stack([slab, slabs - 1 - slab, column, columns - 1 - column])
    field, up, down, right, left = splat(inbox.reshape(-1, LANES))
    below = passed_along(up, "gx", 1)
    above = passed_along(down, "gx", -1)
    right, left = join(edges, below, above, right, left)
    before = passed_along(right, "yz", 1)
    after = passed_along(left, "yz", -1)
    return finish(edges, field, below, above, before, after)


def solution(mesh):
    return jax.shard_map(
        shards,
        mesh=mesh,
        in_specs=(
            P(("gx", "yz"), None),
            P(("gx", "yz"), None),
            P(("gx", "yz"), None, None),
            P(("gx", "yz"), None, None),
            P(("gx", "yz"), None),
            P(("gx", "yz")),
        ),
        out_specs=(P("gx", "yz", None), P("gx", "yz", None)),
        check_vma=False,
    )
```

time: 90 us -> 74.4 us (0.83)
  the two profiles are of different devices: /device:TPU:40 before, /device:TPU:30 now
where the time goes in v3:
time: 74.4 us; the launch traced here: 74.1 us
  waiting for transfers between devices  36.1 us (49%)
  Pallas kernels  20.8 us (28%)
  starting transfers between devices  15.8 us (21%)
  between operations  1.32 us (2%)
    all_to_all x1, waiting for transfers between devices, shards(): lax.all_to_all(outbox, ('gx', 'yz'), split_axis=0, concat_axis=0, tiled=T...  27.9 us
    pallas_call x1, Pallas kernels, splat(): pl.pallas_call(splat_kernel, out_shape=tuple((jax.ShapeDtypeStruct(shape,...  13.8 us
    all_to_all x1, starting transfers between devices, shards(): lax.all_to_all(outbox, ('gx', 'yz'), split_axis=0, concat_axis=0, tiled=T...  9.93 us
    ppermute x4, waiting for transfers between devices, passed_along(): lax.ppermute(value, axis, [(source, (source + steps) % count) for source...  8.25 us
    ppermute x4, starting transfers between devices, passed_along(): lax.ppermute(value, axis, [(source, (source + steps) % count) for source...  5.87 us
    pallas_call x1, Pallas kernels, dispatch(): pl.pallas_call(dispatch_kernel, out_shape=jax.ShapeDtypeStruct((bricks *...  5.28 us
  transfers between devices with their start and end apart: 5, of which 4 were waited for; matrix products, arithmetic and copies ran while one was open for 0% of the time, Pallas kernels for 0%

profile of v3, /device:TPU:30, one launch (start us, length us, event | category | flops | bytes accessed | tf_op | source)
XLA Modules:
  0.0 74.1 jit_solution(3923974904091352568)
XLA Ops:
  1.3 5.3 %dispatch.1 = f32[256,16,128]{2,1,0:T(8,128)} custom-call(s32[128]{0:T(128)} %bitcast.11, s32[1]{0:T(128)S(6)} %copy.8.count_ref, s32[128,256]{1,0:T(8,128)} %offset_ref.1, f32[3,128,256]{2,1,0:T(8,128)} %bitcast.9, f32[3,128,256]{2,1,0:T(8,128)} %bitcast.10, f32[128,256]{1,0:T(8,128)} %weight_ref.1), custom_call_target="tpu_custom_call" | custom-call | tf_op jit(solution)/shard_map/dispatch/pallas_call | solution.py:63
  6.6 9.9 %all-to-all-start = ((f32[256,16,128]{2,1,0:T(8,128)}), f32[256,16,128]{2,1,0:T(8,128)S(1)}, u32[]{:S(2)}, u32[]{:S(2)}) async-start(f32[256,16,128]{2,1,0:T(8,128)} %dispatch.1), calls=%async_computation | async-start | bytes 4194304 | tf_op jit(solution)/shard_map/all_to_all | solution.py:300
  16.5 27.9 %all-to-all-done = f32[256,16,128]{2,1,0:T(8,128)S(1)} async-done(((f32[256,16,128]{2,1,0:T(8,128)}), f32[256,16,128]{2,1,0:T(8,128)S(1)}, u32[]{:S(2)}, u32[]{:S(2)}) %all-to-all-start) | async-done | bytes 2097184 | tf_op jit(solution)/shard_map/all_to_all | solution.py:300
  44.4 13.8 %splat.1 = (f32[2,4,8,128]{3,2,1,0:T(8,128)S(1)}, f32[24,128]{1,0:T(8,128)S(1)}, f32[24,128]{1,0:T(8,128)S(1)}, f32[8,128]{1,0:T(8,128)S(1)}, f32[8,128]{1,0:T(8,128)S(1)}) custom-call(f32[4096,128]{1,0:T(8,128)S(1)} %bitcast.8), custom_call_target="tpu_custom_call" | custom-call | tf_op jit(solution)/shard_map/splat/pallas_call | solution.py:218
  58.2 0.0 collective-permute-start
  58.2 2.9 %collective-permute-start.1 = (f32[24,128]{1,0:T(8,128)S(1)}, f32[24,128]{1,0:T(8,128)S(1)}, u32[]{:S(2)}, u32[]{:S(2)}) collective-permute-start(f32[24,128]{1,0:T(8,128)S(1)} %get-tuple-element.11), channel_id=1, source_target_pairs={{0,112},{16,0},{32,16},{48,32},{64,48},{80,64},{96,80},{112,96},{1... | collective-permute-start | bytes 36872 | tf_op jit(solution)/shard_map/ppermute | solution.py:26
  61.2 0.1 pad_add_fusion.edge_ref
  61.3 1.3 %collective-permute-done.below_ref = f32[24,128]{1,0:T(8,128)S(1)} collective-permute-done((f32[24,128]{1,0:T(8,128)S(1)}, f32[24,128]{1,0:T(8,128)S(1)}, u32[]{:S(2)}, u32[]{:S(2)}) %collective-permute-start) | collective-permute-done | bytes 12320 | tf_op jit(solution)/shard_map/ppermute | solution.py:26
  62.6 0.0 collective-permute-done.1.above_ref
  62.6 0.6 join.1
  63.1 2.9 %collective-permute-start.2 = (f32[8,128]{1,0:T(8,128)S(1)}, f32[8,128]{1,0:T(8,128)S(1)}, u32[]{:S(2)}, u32[]{:S(2)}) collective-permute-start(f32[8,128]{1,0:T(8,128)S(1)} %get-tuple-element.14), channel_id=1, source_target_pairs={{0,1},{1,2},{2,3},{3,4},{4,5},{5,6},{6,7},{7,8},{8,9},{9,10},{10,1... | collective-permute-start | bytes 12296 | tf_op jit(solution)/shard_map/ppermute | solution.py:26
  66.0 0.0 collective-permute-start.3
  66.0 1.3 %collective-permute-done.2.before_ref = f32[8,128]{1,0:T(8,128)S(1)} collective-permute-done((f32[8,128]{1,0:T(8,128)S(1)}, f32[8,128]{1,0:T(8,128)S(1)}, u32[]{:S(2)}, u32[]{:S(2)}) %collective-permute-start.2) | collective-permute-done | bytes 4128 | tf_op jit(solution)/shard_map/ppermute | solution.py:26
  67.4 5.6 %collective-permute-done.3.after_ref = f32[8,128]{1,0:T(8,128)S(1)} collective-permute-done((f32[8,128]{1,0:T(8,128)S(1)}, f32[8,128]{1,0:T(8,128)S(1)}, u32[]{:S(2)}, u32[]{:S(2)}) %collective-permute-start.3) | collective-permute-done | bytes 4128 | tf_op jit(solution)/shard_map/ppermute | solution.py:26
  73.0 1.2 %finish.1 = (f32[4,8,128]{2,1,0:T(8,128)}, f32[4,8,128]{2,1,0:T(8,128)}) custom-call(s32[4]{0:T(128)S(1)} %pad_add_fusion.edge_ref, f32[2,4,8,128]{3,2,1,0:T(8,128)S(1)} %get-tuple-element.9.field_ref, f32[24,128]{1,0:T(8,128)S(1)} %collective-permute-done.below_ref, f32[24,128]{1,0:T(8,128)S(1)} %collective-permute-done.1.above_ref, ...), custom_call_target="tpu_custom_call" | custom-call | tf_op jit(solution)/shard_map/finish/pallas_call | solution.py:279
Async XLA Ops:
  6.6 37.8 %all-to-all-start = ((f32[256,16,128]{2,1,0:T(8,128)}), f32[256,16,128]{2,1,0:T(8,128)S(1)}, u32[]{:S(2)}, u32[]{:S(2)}) async-start(f32[256,16,128]{2,1,0:T(8,128)} %dispatch.1), calls=%async_computation | async-start | bytes 4194304 | tf_op jit(solution)/shard_map/all_to_all | solution.py:300
  58.2 4.3 %collective-permute-start = (f32[24,128]{1,0:T(8,128)S(1)}, f32[24,128]{1,0:T(8,128)S(1)}, u32[]{:S(2)}, u32[]{:S(2)}) collective-permute-start(f32[24,128]{1,0:T(8,128)S(1)} %get-tuple-element.10), channel_id=1, source_target_pairs={{0,16},{16,32},{32,48},{48,64},{64,80},{80,96},{96,112},{112,0},{1... | collective-permute-start | bytes 36872 | tf_op jit(solution)/shard_map/ppermute | solution.py:26
  58.2 4.3 %collective-permute-start.1 = (f32[24,128]{1,0:T(8,128)S(1)}, f32[24,128]{1,0:T(8,128)S(1)}, u32[]{:S(2)}, u32[]{:S(2)}) collective-permute-start(f32[24,128]{1,0:T(8,128)S(1)} %get-tuple-element.11), channel_id=1, source_target_pairs={{0,112},{16,0},{32,16},{48,32},{64,48},{80,64},{96,80},{112,96},{1... | collective-permute-start | bytes 36872 | tf_op jit(solution)/shard_map/ppermute | solution.py:26
  63.1 4.2 %collective-permute-start.2 = (f32[8,128]{1,0:T(8,128)S(1)}, f32[8,128]{1,0:T(8,128)S(1)}, u32[]{:S(2)}, u32[]{:S(2)}) collective-permute-start(f32[8,128]{1,0:T(8,128)S(1)} %get-tuple-element.14), channel_id=1, source_target_pairs={{0,1},{1,2},{2,3},{3,4},{4,5},{5,6},{6,7},{7,8},{8,9},{9,10},{10,1... | collective-permute-start | bytes 12296 | tf_op jit(solution)/shard_map/ppermute | solution.py:26
  66.0 6.9 %collective-permute-start.3 = (f32[8,128]{1,0:T(8,128)S(1)}, f32[8,128]{1,0:T(8,128)S(1)}, u32[]{:S(2)}, u32[]{:S(2)}) collective-permute-start(f32[8,128]{1,0:T(8,128)S(1)} %get-tuple-element.15), channel_id=1, source_target_pairs={{0,15},{1,0},{2,1},{3,2},{4,3},{5,4},{6,5},{7,6},{8,7},{9,8},{10,9... | collective-permute-start | bytes 12296 | tf_op jit(solution)/shard_map/ppermute | solution.py:26

commit v4 on v3

--- a/solution.py
+++ b/solution.py
@@ -11,7 +11,7 @@
 CAP = 2
 LANES = 128
 GROUP = 8
-UNROLL = 8
+UNROLL = 16
 PLANES = (BX + 2) * BY
 ENDS = 16
 ROWS = PLANES + ENDS
@@ -26,46 +26,72 @@
     return lax.ppermute(value, axis, [(source, (source + steps) % count) for source in range(count)])
 
 
-def dispatch_kernel(ids_ref, count_ref, offset_ref, frac_ref, normal_ref, weight_ref, out_ref, seen_ref):
-    slots = out_ref.shape[0]
-
-    def clear(i, _):
-        out_ref[pl.ds(i * 8, 8)] = jnp.zeros((8,) + out_ref.shape[1:], jnp.float32)
-        return 0
-
-    lax.fori_loop(0, slots // 8, clear, 0)
+def dispatch_kernel(ids_ref, count_ref, offset_hbm, frac_hbm, normal_hbm, weight_hbm, out_hbm, *scratch):
+    offset_ref, frac_ref, normal_ref, weight_ref, out_ref, seen_ref, slot_ref, sems = scratch
+    tiles, slots = ids_ref.shape[0], out_hbm.shape[0]
+    pairs = ((offset_hbm, offset_ref), (frac_hbm, frac_ref), (normal_hbm, normal_ref), (weight_hbm, weight_ref))
+    loads = [pltpu.make_async_copy(source, target, sems.at[i]) for i, (source, target) in enumerate(pairs)]
+    for load in loads:
+        load.start()
 
     def reset(i, _):
         seen_ref[i] = 0
         return 0
 
-    lax.fori_loop(0, seen_ref.shape[0], reset, 0)
-
-    def place(t, _):
-        brick = ids_ref[t]
-        rank = seen_ref[brick]
-        seen_ref[brick] = rank + 1
-        slot = brick * CAP + jnp.minimum(rank, CAP - 1)
-        here = pl.ds(t, 1)
+    lax.fori_loop(0, seen_ref.shape[0], reset, 0, unroll=16)
+
+    def choose(i, _):
+        for j in range(8):
+            t = 8 * i + j
+            brick = ids_ref[t]
+            rank = seen_ref[brick]
+            seen_ref[brick] = rank + 1
+            slot_ref[t] = jnp.where(t < count_ref[0], brick * CAP + jnp.minimum(rank, CAP - 1), slots)
+            out_ref[pl.ds(2 * t, 2)] = jnp.zeros((2,) + out_ref.shape[1:], jnp.float32)
+        return 0
+
+    lax.fori_loop(0, tiles // 8, choose, 0)
+    for load in loads:
+        load.wait()
+
+    def place(i, _):
+        here = pl.ds(pl.multiple_of(8 * i, 8), 8)
         rows = [frac_ref[k, here, :] for k in range(3)] + [offset_ref[here, :].astype(jnp.float32)]
         rows += [normal_ref[k, here, :] for k in range(3)] + [weight_ref[here, :]]
-        for half in range(out_ref.shape[1] // 8):
-            for k, row in enumerate(rows):
-                out_ref[slot, 8 * half + k : 8 * half + k + 1, :] = row[:, LANES * half : LANES * half + LANES]
+        for j in range(8):
+            slot = slot_ref[8 * i + j]
+            for half in range(out_ref.shape[1] // 8):
+                for k, row in enumerate(rows):
+                    piece = row[j : j + 1, LANES * half : LANES * half + LANES]
+                    out_ref[slot, 8 * half + k : 8 * half + k + 1, :] = piece
         return 0
 
-    lax.fori_loop(0, jnp.minimum(count_ref[0], ids_ref.shape[0]), place, 0)
+    lax.fori_loop(0, tiles // 8, place, 0)
+    store = pltpu.make_async_copy(out_ref.at[pl.ds(0, slots)], out_hbm, sems.at[len(pairs)])
+    store.start()
+    store.wait()
 
 
 def dispatch(ids, count, offset, frac, normal, weight, bricks):
     smem = pl.BlockSpec(memory_space=pltpu.SMEM)
-    vmem = pl.BlockSpec(memory_space=pltpu.VMEM)
+    hbm = pl.BlockSpec(memory_space=pltpu.HBM)
+    block = (8 * offset.shape[1] // LANES, LANES)
+    slots = bricks * CAP
     return pl.pallas_call(
         dispatch_kernel,
-        out_shape=jax.ShapeDtypeStruct((bricks * CAP, 8 * offset.shape[1] // LANES, LANES), jnp.float32),
-        in_specs=[smem, smem, vmem, vmem, vmem, vmem],
-        out_specs=vmem,
-        scratch_shapes=[pltpu.SMEM((bricks,), jnp.int32)],
+        out_shape=jax.ShapeDtypeStruct((slots,) + block, jnp.float32),
+        in_specs=[smem, smem, hbm, hbm, hbm, hbm],
+        out_specs=hbm,
+        scratch_shapes=[
+            pltpu.VMEM(offset.shape, jnp.int32),
+            pltpu.VMEM(frac.shape, jnp.float32),
+            pltpu.VMEM(normal.shape, jnp.float32),
+            pltpu.VMEM(weight.shape, jnp.float32),
+            pltpu.VMEM((slots + 1,) + block, jnp.float32),
+            pltpu.SMEM((bricks,), jnp.int32),
+            pltpu.SMEM(ids.shape, jnp.int32),
+            pltpu.SemaphoreType.DMA((5,)),
+        ],
         name="dispatch",
     )(ids, count, offset, frac, normal, weight)
 
@@ -174,18 +200,22 @@
 
     acc_ref[...] = jnp.zeros_like(acc_ref)
 
+    for u in range(UNROLL):
+        prepare(inbox_ref, u * GROUP, row_ref.at[u], side_ref.at[u])
+
     def body(i, _):
+        acc = acc_ref[...]
+        coming = jnp.minimum(i + 1, steps - 1) * batch
         for u in range(UNROLL):
-            prepare(inbox_ref, i * batch + u * GROUP, row_ref.at[u], side_ref.at[u])
-        acc = acc_ref[...]
-        for pair in range(batch // 2):
-            sides = [build(row_ref.at[k // GROUP], side_ref.at[k // GROUP], k % GROUP) for k in (2 * pair, 2 * pair + 1)]
-            acc = acc + lax.dot_general(
-                jnp.concatenate([a for a, _ in sides], axis=1),
-                jnp.concatenate([z for _, z in sides], axis=1),
-                (((1,), (1,)), ((), ())),
-                preferred_element_type=jnp.float32,
-            )
+            for pair in range(GROUP // 2):
+                sides = [build(row_ref.at[u], side_ref.at[u], k) for k in (2 * pair, 2 * pair + 1)]
+                acc = acc + lax.dot_general(
+                    jnp.concatenate([a for a, _ in sides], axis=1),
+                    jnp.concatenate([z for _, z in sides], axis=1),
+                    (((1,), (1,)), ((), ())),
+                    preferred_element_type=jnp.float32,
+                )
+            prepare(inbox_ref, coming + u * GROUP, row_ref.at[u], side_ref.at[u])
         acc_ref[...] = acc
         return 0
 

time: 74.4 us -> 72.3 us (0.972)
  Pallas kernels: 20.8 us -> 18.4 us
    pallas_call x1, Pallas kernels: 5.28 us -> 3.9 us  [dispatch(): pl.pallas_call(dispatch_kernel, out_shape=jax.ShapeDtypeStruct((slots,) +...]
    pallas_call x1, Pallas kernels: 13.8 us -> 12.8 us  [splat(): pl.pallas_call(splat_kernel, out_shape=tuple((jax.ShapeDtypeStruct(shape,...]
where the time goes in v4:
time: 72.3 us; the launch traced here: 72.1 us
  waiting for transfers between devices  36.1 us (50%)
  Pallas kernels  18.4 us (25%)
  starting transfers between devices  16.1 us (22%)
  between operations  1.33 us (2%)
    all_to_all x1, waiting for transfers between devices, shards(): lax.all_to_all(outbox, ('gx', 'yz'), split_axis=0, concat_axis=0, tiled=T...  27.9 us
    pallas_call x1, Pallas kernels, splat(): pl.pallas_call(splat_kernel, out_shape=tuple((jax.ShapeDtypeStruct(shape,...  12.8 us
    all_to_all x1, starting transfers between devices, shards(): lax.all_to_all(outbox, ('gx', 'yz'), split_axis=0, concat_axis=0, tiled=T...  10.2 us
    ppermute x4, waiting for transfers between devices, passed_along(): lax.ppermute(value, axis, [(source, (source + steps) % count) for source...  8.25 us
    ppermute x4, starting transfers between devices, passed_along(): lax.ppermute(value, axis, [(source, (source + steps) % count) for source...  5.88 us
    pallas_call x1, Pallas kernels, dispatch(): pl.pallas_call(dispatch_kernel, out_shape=jax.ShapeDtypeStruct((slots,) +...  3.9 us
  transfers between devices with their start and end apart: 5, of which 4 were waited for; matrix products, arithmetic and copies ran while one was open for 0% of the time, Pallas kernels for 0%

profile of v4, /device:TPU:30, one launch (start us, length us, event | category | flops | bytes accessed | tf_op | source)
XLA Modules:
  0.0 72.1 jit_solution(6210000252578099526)
XLA Ops:
  1.3 3.9 %dispatch.1 = f32[256,16,128]{2,1,0:T(8,128)} custom-call(s32[128]{0:T(128)} %bitcast.11, s32[1]{0:T(128)S(6)} %copy.8.count_ref, s32[128,256]{1,0:T(8,128)} %offset_hbm.1, f32[3,128,256]{2,1,0:T(8,128)} %bitcast.9, f32[3,128,256]{2,1,0:T(8,128)} %bitcast.10, f32[128,256]{1,0:T(8,128)} %weight_hbm.1), custom_call_target="tpu_custom_call" | custom-call | tf_op jit(solution)/shard_map/dispatch/pallas_call | solution.py:80
  5.2 10.2 %all-to-all-start = ((f32[256,16,128]{2,1,0:T(8,128)}), f32[256,16,128]{2,1,0:T(8,128)S(1)}, u32[]{:S(2)}, u32[]{:S(2)}) async-start(f32[256,16,128]{2,1,0:T(8,128)} %dispatch.1), calls=%async_computation | async-start | bytes 4194304 | tf_op jit(solution)/shard_map/all_to_all | solution.py:330
  15.4 27.9 %all-to-all-done = f32[256,16,128]{2,1,0:T(8,128)S(1)} async-done(((f32[256,16,128]{2,1,0:T(8,128)}), f32[256,16,128]{2,1,0:T(8,128)S(1)}, u32[]{:S(2)}, u32[]{:S(2)}) %all-to-all-start) | async-done | bytes 2097184 | tf_op jit(solution)/shard_map/all_to_all | solution.py:330
  43.3 12.8 %splat.1 = (f32[2,4,8,128]{3,2,1,0:T(8,128)S(1)}, f32[24,128]{1,0:T(8,128)S(1)}, f32[24,128]{1,0:T(8,128)S(1)}, f32[8,128]{1,0:T(8,128)S(1)}, f32[8,128]{1,0:T(8,128)S(1)}) custom-call(f32[4096,128]{1,0:T(8,128)S(1)} %bitcast.8), custom_call_target="tpu_custom_call" | custom-call | tf_op jit(solution)/shard_map/splat/pallas_call | solution.py:248
  56.1 0.0 collective-permute-start
  56.1 2.9 %collective-permute-start.1 = (f32[24,128]{1,0:T(8,128)S(1)}, f32[24,128]{1,0:T(8,128)S(1)}, u32[]{:S(2)}, u32[]{:S(2)}) collective-permute-start(f32[24,128]{1,0:T(8,128)S(1)} %get-tuple-element.11), channel_id=1, source_target_pairs={{0,112},{16,0},{32,16},{48,32},{64,48},{80,64},{96,80},{112,96},{1... | collective-permute-start | bytes 36872 | tf_op jit(solution)/shard_map/ppermute | solution.py:26
  59.1 0.1 pad_add_fusion.edge_ref
  59.2 1.3 %collective-permute-done.below_ref = f32[24,128]{1,0:T(8,128)S(1)} collective-permute-done((f32[24,128]{1,0:T(8,128)S(1)}, f32[24,128]{1,0:T(8,128)S(1)}, u32[]{:S(2)}, u32[]{:S(2)}) %collective-permute-start) | collective-permute-done | bytes 12320 | tf_op jit(solution)/shard_map/ppermute | solution.py:26
  60.4 0.0 collective-permute-done.1.above_ref
  60.5 0.6 join.1
  61.0 2.9 %collective-permute-start.2 = (f32[8,128]{1,0:T(8,128)S(1)}, f32[8,128]{1,0:T(8,128)S(1)}, u32[]{:S(2)}, u32[]{:S(2)}) collective-permute-start(f32[8,128]{1,0:T(8,128)S(1)} %get-tuple-element.14), channel_id=1, source_target_pairs={{0,1},{1,2},{2,3},{3,4},{4,5},{5,6},{6,7},{7,8},{8,9},{9,10},{10,1... | collective-permute-start | bytes 12296 | tf_op jit(solution)/shard_map/ppermute | solution.py:26
  64.0 0.0 collective-permute-start.3
  64.0 1.3 %collective-permute-done.2.before_ref = f32[8,128]{1,0:T(8,128)S(1)} collective-permute-done((f32[8,128]{1,0:T(8,128)S(1)}, f32[8,128]{1,0:T(8,128)S(1)}, u32[]{:S(2)}, u32[]{:S(2)}) %collective-permute-start.2) | collective-permute-done | bytes 4128 | tf_op jit(solution)/shard_map/ppermute | solution.py:26
  65.3 5.6 %collective-permute-done.3.after_ref = f32[8,128]{1,0:T(8,128)S(1)} collective-permute-done((f32[8,128]{1,0:T(8,128)S(1)}, f32[8,128]{1,0:T(8,128)S(1)}, u32[]{:S(2)}, u32[]{:S(2)}) %collective-permute-start.3) | collective-permute-done | bytes 4128 | tf_op jit(solution)/shard_map/ppermute | solution.py:26
  70.9 1.2 %finish.1 = (f32[4,8,128]{2,1,0:T(8,128)}, f32[4,8,128]{2,1,0:T(8,128)}) custom-call(s32[4]{0:T(128)S(1)} %pad_add_fusion.edge_ref, f32[2,4,8,128]{3,2,1,0:T(8,128)S(1)} %get-tuple-element.9.field_ref, f32[24,128]{1,0:T(8,128)S(1)} %collective-permute-done.below_ref, f32[24,128]{1,0:T(8,128)S(1)} %collective-permute-done.1.above_ref, ...), custom_call_target="tpu_custom_call" | custom-call | tf_op jit(solution)/shard_map/finish/pallas_call | solution.py:309
Async XLA Ops:
  5.2 38.1 %all-to-all-start = ((f32[256,16,128]{2,1,0:T(8,128)}), f32[256,16,128]{2,1,0:T(8,128)S(1)}, u32[]{:S(2)}, u32[]{:S(2)}) async-start(f32[256,16,128]{2,1,0:T(8,128)} %dispatch.1), calls=%async_computation | async-start | bytes 4194304 | tf_op jit(solution)/shard_map/all_to_all | solution.py:330
  56.1 4.3 %collective-permute-start = (f32[24,128]{1,0:T(8,128)S(1)}, f32[24,128]{1,0:T(8,128)S(1)}, u32[]{:S(2)}, u32[]{:S(2)}) collective-permute-start(f32[24,128]{1,0:T(8,128)S(1)} %get-tuple-element.10), channel_id=1, source_target_pairs={{0,16},{16,32},{32,48},{48,64},{64,80},{80,96},{96,112},{112,0},{1... | collective-permute-start | bytes 36872 | tf_op jit(solution)/shard_map/ppermute | solution.py:26
  56.1 4.3 %collective-permute-start.1 = (f32[24,128]{1,0:T(8,128)S(1)}, f32[24,128]{1,0:T(8,128)S(1)}, u32[]{:S(2)}, u32[]{:S(2)}) collective-permute-start(f32[24,128]{1,0:T(8,128)S(1)} %get-tuple-element.11), channel_id=1, source_target_pairs={{0,112},{16,0},{32,16},{48,32},{64,48},{80,64},{96,80},{112,96},{1... | collective-permute-start | bytes 36872 | tf_op jit(solution)/shard_map/ppermute | solution.py:26
  61.0 4.2 %collective-permute-start.2 = (f32[8,128]{1,0:T(8,128)S(1)}, f32[8,128]{1,0:T(8,128)S(1)}, u32[]{:S(2)}, u32[]{:S(2)}) collective-permute-start(f32[8,128]{1,0:T(8,128)S(1)} %get-tuple-element.14), channel_id=1, source_target_pairs={{0,1},{1,2},{2,3},{3,4},{4,5},{5,6},{6,7},{7,8},{8,9},{9,10},{10,1... | collective-permute-start | bytes 12296 | tf_op jit(solution)/shard_map/ppermute | solution.py:26
  64.0 6.9 %collective-permute-start.3 = (f32[8,128]{1,0:T(8,128)S(1)}, f32[8,128]{1,0:T(8,128)S(1)}, u32[]{:S(2)}, u32[]{:S(2)}) collective-permute-start(f32[8,128]{1,0:T(8,128)S(1)} %get-tuple-element.15), channel_id=1, source_target_pairs={{0,15},{1,0},{2,1},{3,2},{4,3},{5,4},{6,5},{7,6},{8,7},{9,8},{10,9... | collective-permute-start | bytes 12296 | tf_op jit(solution)/shard_map/ppermute | solution.py:26

commit v5 on v4

--- a/solution.py
+++ b/solution.py
@@ -12,6 +12,8 @@
 LANES = 128
 GROUP = 8
 UNROLL = 16
+AHEAD = 2
+SLOTS = 16
 PLANES = (BX + 2) * BY
 ENDS = 16
 ROWS = PLANES + ENDS
@@ -120,6 +122,10 @@
     def channel(c):
         return inbox_ref[pl.ds(first * 8 + c, GROUP, stride=8), :]
 
+    def put(i, s, v):
+        for h in range(2):
+            side_ref[i, h, 4 * s : 4 * s + 4, :] = v[4 * h : 4 * h + 4]
+
     offset = channel(3).astype(jnp.int32)
     weights, slopes = spline(channel(0))
     cell = lax.shift_right_logical(offset, 10)
@@ -136,10 +142,10 @@
             yv, ys = y_value[BY + e], y_slope[BY + e]
             ends = (parts[0] * yv + parts[1] * ys, parts[2] * yv, parts[3] * yv)
             for k in range(3):
-                side_ref[2 * k + e, GROUP * r : GROUP * r + GROUP, :] = ends[k]
+                put(2 * k + e, r, ends[k])
     for s in range(BY):
-        side_ref[6, GROUP * s : GROUP * s + GROUP, :] = y_value[s]
-        side_ref[7, GROUP * s : GROUP * s + GROUP, :] = y_slope[s]
+        put(6, s, y_value[s])
+        put(7, s, y_slope[s])
     weights, slopes = spline(channel(2))
     cell = offset & 127
     rows = weights + slopes + [(cell & 15).astype(jnp.float32), lax.shift_right_logical(cell, 4).astype(jnp.float32)]
@@ -156,7 +162,7 @@
         return jnp.concatenate([v, v], axis=0).astype(jnp.bfloat16)
 
     def side(i):
-        return side_ref[i, pl.ds(unit, 8, stride=GROUP), :]
+        return side_ref[i, unit // 4, pl.ds(unit % 4, 8, stride=4), :]
 
     y_value, y_slope = side(6), side(7)
     left = [[], [], []]
@@ -200,22 +206,26 @@
 
     acc_ref[...] = jnp.zeros_like(acc_ref)
 
-    for u in range(UNROLL):
-        prepare(inbox_ref, u * GROUP, row_ref.at[u], side_ref.at[u])
+    def ready(group, slot):
+        group = jnp.minimum(group, steps * UNROLL - 1)
+        prepare(inbox_ref, group * GROUP, row_ref.at[slot], side_ref.at[slot])
+
+    for u in range(AHEAD):
+        ready(u, u)
 
     def body(i, _):
         acc = acc_ref[...]
-        coming = jnp.minimum(i + 1, steps - 1) * batch
         for u in range(UNROLL):
+            slot = u % SLOTS
             for pair in range(GROUP // 2):
-                sides = [build(row_ref.at[u], side_ref.at[u], k) for k in (2 * pair, 2 * pair + 1)]
+                sides = [build(row_ref.at[slot], side_ref.at[slot], k) for k in (2 * pair, 2 * pair + 1)]
                 acc = acc + lax.dot_general(
                     jnp.concatenate([a for a, _ in sides], axis=1),
                     jnp.concatenate([z for _, z in sides], axis=1),
                     (((1,), (1,)), ((), ())),
                     preferred_element_type=jnp.float32,
                 )
-            prepare(inbox_ref, coming + u * GROUP, row_ref.at[u], side_ref.at[u])
+            ready(i * UNROLL + u + AHEAD, (u + AHEAD) % SLOTS)
         acc_ref[...] = acc
         return 0
 
@@ -252,8 +262,8 @@
         out_specs=(vmem,) * len(shapes),
         scratch_shapes=[
             pltpu.VMEM((3 * ROWS, 2 * BZ), jnp.float32),
-            pltpu.VMEM((UNROLL, ROW_COUNT, GROUP, LANES), jnp.float32),
-            pltpu.VMEM((UNROLL, SIDES, 8 * GROUP, LANES), jnp.float32),
+            pltpu.VMEM((SLOTS, ROW_COUNT, GROUP, LANES), jnp.float32),
+            pltpu.VMEM((SLOTS, SIDES, 2, 4 * 8, LANES), jnp.float32),
         ],
         compiler_params=pltpu.CompilerParams(vmem_limit_bytes=16 * 1024 * 1024),
         name="splat",

time: 72.3 us -> 71.3 us (0.986)
  Pallas kernels: 18.4 us -> 17.5 us
    pallas_call x1, Pallas kernels: 12.8 us -> 11.8 us  [splat(): pl.pallas_call(splat_kernel, out_shape=tuple((jax.ShapeDtypeStruct(shape,...]
where the time goes in v5:
time: 71.3 us; the launch traced here: 71.1 us
  waiting for transfers between devices  36.1 us (51%)
  Pallas kernels  17.5 us (25%)
  starting transfers between devices  16.1 us (23%)
  between operations  1.33 us (2%)
    all_to_all x1, waiting for transfers between devices, shards(): lax.all_to_all(outbox, ('gx', 'yz'), split_axis=0, concat_axis=0, tiled=T...  27.9 us
    pallas_call x1, Pallas kernels, splat(): pl.pallas_call(splat_kernel, out_shape=tuple((jax.ShapeDtypeStruct(shape,...  11.8 us
    all_to_all x1, starting transfers between devices, shards(): lax.all_to_all(outbox, ('gx', 'yz'), split_axis=0, concat_axis=0, tiled=T...  10.2 us
    ppermute x4, waiting for transfers between devices, passed_along(): lax.ppermute(value, axis, [(source, (source + steps) % count) for source...  8.25 us
    ppermute x4, starting transfers between devices, passed_along(): lax.ppermute(value, axis, [(source, (source + steps) % count) for source...  5.87 us
    pallas_call x1, Pallas kernels, dispatch(): pl.pallas_call(dispatch_kernel, out_shape=jax.ShapeDtypeStruct((slots,) +...  3.9 us
  transfers between devices with their start and end apart: 5, of which 4 were waited for; matrix products, arithmetic and copies ran while one was open for 0% of the time, Pallas kernels for 0%

profile of v5, /device:TPU:30, one launch (start us, length us, event | category | flops | bytes accessed | tf_op | source)
XLA Modules:
  0.0 71.1 jit_solution(13923963201718467351)
XLA Ops:
  1.3 3.9 %dispatch.1 = f32[256,16,128]{2,1,0:T(8,128)} custom-call(s32[128]{0:T(128)} %bitcast.11, s32[1]{0:T(128)S(6)} %copy.8.count_ref, s32[128,256]{1,0:T(8,128)} %offset_hbm.1, f32[3,128,256]{2,1,0:T(8,128)} %bitcast.9, f32[3,128,256]{2,1,0:T(8,128)} %bitcast.10, f32[128,256]{1,0:T(8,128)} %weight_hbm.1), custom_call_target="tpu_custom_call" | custom-call | tf_op jit(solution)/shard_map/dispatch/pallas_call | solution.py:82
  5.2 10.2 %all-to-all-start = ((f32[256,16,128]{2,1,0:T(8,128)}), f32[256,16,128]{2,1,0:T(8,128)S(1)}, u32[]{:S(2)}, u32[]{:S(2)}) async-start(f32[256,16,128]{2,1,0:T(8,128)} %dispatch.1), calls=%async_computation | async-start | bytes 4194304 | tf_op jit(solution)/shard_map/all_to_all | solution.py:340
  15.4 27.9 %all-to-all-done = f32[256,16,128]{2,1,0:T(8,128)S(1)} async-done(((f32[256,16,128]{2,1,0:T(8,128)}), f32[256,16,128]{2,1,0:T(8,128)S(1)}, u32[]{:S(2)}, u32[]{:S(2)}) %all-to-all-start) | async-done | bytes 2097184 | tf_op jit(solution)/shard_map/all_to_all | solution.py:340
  43.3 11.8 %splat.1 = (f32[2,4,8,128]{3,2,1,0:T(8,128)S(1)}, f32[24,128]{1,0:T(8,128)S(1)}, f32[24,128]{1,0:T(8,128)S(1)}, f32[8,128]{1,0:T(8,128)S(1)}, f32[8,128]{1,0:T(8,128)S(1)}) custom-call(f32[4096,128]{1,0:T(8,128)S(1)} %bitcast.8), custom_call_target="tpu_custom_call" | custom-call | tf_op jit(solution)/shard_map/splat/pallas_call | solution.py:258
  55.2 0.0 collective-permute-start
  55.2 2.9 %collective-permute-start.1 = (f32[24,128]{1,0:T(8,128)S(1)}, f32[24,128]{1,0:T(8,128)S(1)}, u32[]{:S(2)}, u32[]{:S(2)}) collective-permute-start(f32[24,128]{1,0:T(8,128)S(1)} %get-tuple-element.11), channel_id=1, source_target_pairs={{0,112},{16,0},{32,16},{48,32},{64,48},{80,64},{96,80},{112,96},{1... | collective-permute-start | bytes 36872 | tf_op jit(solution)/shard_map/ppermute | solution.py:28
  58.1 0.1 pad_add_fusion.edge_ref
  58.2 1.3 %collective-permute-done.below_ref = f32[24,128]{1,0:T(8,128)S(1)} collective-permute-done((f32[24,128]{1,0:T(8,128)S(1)}, f32[24,128]{1,0:T(8,128)S(1)}, u32[]{:S(2)}, u32[]{:S(2)}) %collective-permute-start) | collective-permute-done | bytes 12320 | tf_op jit(solution)/shard_map/ppermute | solution.py:28
  59.5 0.0 collective-permute-done.1.above_ref
  59.6 0.6 join.1
  60.1 2.9 %collective-permute-start.2 = (f32[8,128]{1,0:T(8,128)S(1)}, f32[8,128]{1,0:T(8,128)S(1)}, u32[]{:S(2)}, u32[]{:S(2)}) collective-permute-start(f32[8,128]{1,0:T(8,128)S(1)} %get-tuple-element.14), channel_id=1, source_target_pairs={{0,1},{1,2},{2,3},{3,4},{4,5},{5,6},{6,7},{7,8},{8,9},{9,10},{10,1... | collective-permute-start | bytes 12296 | tf_op jit(solution)/shard_map/ppermute | solution.py:28
  63.0 0.0 collective-permute-start.3
  63.0 1.3 %collective-permute-done.2.before_ref = f32[8,128]{1,0:T(8,128)S(1)} collective-permute-done((f32[8,128]{1,0:T(8,128)S(1)}, f32[8,128]{1,0:T(8,128)S(1)}, u32[]{:S(2)}, u32[]{:S(2)}) %collective-permute-start.2) | collective-permute-done | bytes 4128 | tf_op jit(solution)/shard_map/ppermute | solution.py:28
  64.3 5.6 %collective-permute-done.3.after_ref = f32[8,128]{1,0:T(8,128)S(1)} collective-permute-done((f32[8,128]{1,0:T(8,128)S(1)}, f32[8,128]{1,0:T(8,128)S(1)}, u32[]{:S(2)}, u32[]{:S(2)}) %collective-permute-start.3) | collective-permute-done | bytes 4128 | tf_op jit(solution)/shard_map/ppermute | solution.py:28
  69.9 1.2 %finish.1 = (f32[4,8,128]{2,1,0:T(8,128)}, f32[4,8,128]{2,1,0:T(8,128)}) custom-call(s32[4]{0:T(128)S(1)} %pad_add_fusion.edge_ref, f32[2,4,8,128]{3,2,1,0:T(8,128)S(1)} %get-tuple-element.9.field_ref, f32[24,128]{1,0:T(8,128)S(1)} %collective-permute-done.below_ref, f32[24,128]{1,0:T(8,128)S(1)} %collective-permute-done.1.above_ref, ...), custom_call_target="tpu_custom_call" | custom-call | tf_op jit(solution)/shard_map/finish/pallas_call | solution.py:319
Async XLA Ops:
  5.2 38.1 %all-to-all-start = ((f32[256,16,128]{2,1,0:T(8,128)}), f32[256,16,128]{2,1,0:T(8,128)S(1)}, u32[]{:S(2)}, u32[]{:S(2)}) async-start(f32[256,16,128]{2,1,0:T(8,128)} %dispatch.1), calls=%async_computation | async-start | bytes 4194304 | tf_op jit(solution)/shard_map/all_to_all | solution.py:340
  55.2 4.3 %collective-permute-start = (f32[24,128]{1,0:T(8,128)S(1)}, f32[24,128]{1,0:T(8,128)S(1)}, u32[]{:S(2)}, u32[]{:S(2)}) collective-permute-start(f32[24,128]{1,0:T(8,128)S(1)} %get-tuple-element.10), channel_id=1, source_target_pairs={{0,16},{16,32},{32,48},{48,64},{64,80},{80,96},{96,112},{112,0},{1... | collective-permute-start | bytes 36872 | tf_op jit(solution)/shard_map/ppermute | solution.py:28
  55.2 4.3 %collective-permute-start.1 = (f32[24,128]{1,0:T(8,128)S(1)}, f32[24,128]{1,0:T(8,128)S(1)}, u32[]{:S(2)}, u32[]{:S(2)}) collective-permute-start(f32[24,128]{1,0:T(8,128)S(1)} %get-tuple-element.11), channel_id=1, source_target_pairs={{0,112},{16,0},{32,16},{48,32},{64,48},{80,64},{96,80},{112,96},{1... | collective-permute-start | bytes 36872 | tf_op jit(solution)/shard_map/ppermute | solution.py:28
  60.1 4.2 %collective-permute-start.2 = (f32[8,128]{1,0:T(8,128)S(1)}, f32[8,128]{1,0:T(8,128)S(1)}, u32[]{:S(2)}, u32[]{:S(2)}) collective-permute-start(f32[8,128]{1,0:T(8,128)S(1)} %get-tuple-element.14), channel_id=1, source_target_pairs={{0,1},{1,2},{2,3},{3,4},{4,5},{5,6},{6,7},{7,8},{8,9},{9,10},{10,1... | collective-permute-start | bytes 12296 | tf_op jit(solution)/shard_map/ppermute | solution.py:28
  63.0 6.9 %collective-permute-start.3 = (f32[8,128]{1,0:T(8,128)S(1)}, f32[8,128]{1,0:T(8,128)S(1)}, u32[]{:S(2)}, u32[]{:S(2)}) collective-permute-start(f32[8,128]{1,0:T(8,128)S(1)} %get-tuple-element.15), channel_id=1, source_target_pairs={{0,15},{1,0},{2,1},{3,2},{4,3},{5,4},{6,5},{7,6},{8,7},{9,8},{10,9... | collective-permute-start | bytes 12296 | tf_op jit(solution)/shard_map/ppermute | solution.py:28

commit v6 on v5

--- a/solution.py
+++ b/solution.py
@@ -11,9 +11,9 @@
 CAP = 2
 LANES = 128
 GROUP = 8
-UNROLL = 16
-AHEAD = 2
-SLOTS = 16
+UNROLL = 32
+AHEAD = 1
+SLOTS = 32
 PLANES = (BX + 2) * BY
 ENDS = 16
 ROWS = PLANES + ENDS
@@ -296,34 +296,29 @@
     )(edges, below, above, right, left)
 
 
-def finish_kernel(edge_ref, field_ref, below_ref, above_ref, before_ref, after_ref, rhs_ref, screen_ref):
-    for k, ref in enumerate((rhs_ref, screen_ref)):
+def widen_kernel(edge_ref, field_ref, below_ref, above_ref, out_ref):
+    for k in range(2):
         for r in range(BX):
             plane = field_ref[k, r]
             if r == 0:
                 plane = plane + jnp.where(edge_ref[0] == 0, 0.0, below_ref[BY * k : BY * k + BY, :])
             if r == BX - 1:
                 plane = plane + jnp.where(edge_ref[1] == 0, 0.0, above_ref[BY * k : BY * k + BY, :])
-            ref[r] = plane
-            at = BX * k + r
-            before = jnp.where(edge_ref[2] == 0, 0.0, before_ref[at : at + 1, :])
-            after = jnp.where(edge_ref[3] == 0, 0.0, after_ref[at : at + 1, :])
-            ref[r, 0:1, :] = ref[r, 0:1, :] + before
-            ref[r, BY - 1 : BY, :] = ref[r, BY - 1 : BY, :] + after
-
-
-def finish(edges, field, below, above, before, after):
+            out_ref[k, r] = plane
+
+
+def widen(edges, field, below, above):
     smem = pl.BlockSpec(memory_space=pltpu.SMEM)
     vmem = pl.BlockSpec(memory_space=pltpu.VMEM)
-    shape = jax.ShapeDtypeStruct((BX, BY, BZ), jnp.float32)
     return pl.pallas_call(
-        finish_kernel,
-        out_shape=(shape, shape),
-        in_specs=[smem] + [vmem] * 5,
-        out_specs=(vmem, vmem),
+        widen_kernel,
+        out_shape=jax.ShapeDtypeStruct(field.shape, jnp.float32),
+        in_specs=[smem] + [vmem] * 3,
+        out_specs=vmem,
+        cost_estimate=pl.CostEstimate(flops=20000000, bytes_accessed=100000, transcendentals=0),
         compiler_params=pltpu.CompilerParams(vmem_limit_bytes=4 * 1024 * 1024),
-        name="finish",
-    )(edges, field, below, above, before, after)
+        name="widen",
+    )(edges, field, below, above)
 
 
 def shards(brick_ids, voxel_offset, fractions, normals, point_weight, tile_count):
@@ -346,7 +341,14 @@
     right, left = join(edges, below, above, right, left)
     before = passed_along(right, "yz", 1)
     after = passed_along(left, "yz", -1)
-    return finish(edges, field, below, above, before, after)
+    field = widen(edges, field, below, above)
+    row = lax.broadcasted_iota(jnp.int32, (1, 1, BY, 1), 2)
+    first = (row == 0) & (column > 0)
+    last = (row == BY - 1) & (column < columns - 1)
+    before = jnp.where(first, before.reshape(2, BX, 1, BZ), 0.0)
+    after = jnp.where(last, after.reshape(2, BX, 1, BZ), 0.0)
+    total = field + before + after
+    return total[0], total[1]
 
 
 def solution(mesh):

time: 71.3 us -> 70.5 us (0.989)
  Pallas kernels: 17.5 us -> 16.5 us
  transfers between devices with their start and end apart: 5 -> 5, of which waited for: 4 -> 4; matrix products, arithmetic and copies ran while one was open for 0% -> 0% of each run, Pallas kernels for 0% -> 1%
where the time goes in v6:
time: 70.5 us; the launch traced here: 70.3 us
  waiting for transfers between devices  35.6 us (50%)
  Pallas kernels  16.5 us (23%)
  starting transfers between devices  16.1 us (23%)
  between operations  1.34 us (2%)
    all_to_all x1, waiting for transfers between devices, shards(): lax.all_to_all(outbox, ('gx', 'yz'), split_axis=0, concat_axis=0, tiled=T...  27.9 us
    pallas_call x1, Pallas kernels, splat(): pl.pallas_call(splat_kernel, out_shape=tuple((jax.ShapeDtypeStruct(shape,...  11.5 us
    all_to_all x1, starting transfers between devices, shards(): lax.all_to_all(outbox, ('gx', 'yz'), split_axis=0, concat_axis=0, tiled=T...  10.2 us
    ppermute x4, waiting for transfers between devices, passed_along(): lax.ppermute(value, axis, [(source, (source + steps) % count) for source...  7.69 us
    ppermute x4, starting transfers between devices, passed_along(): lax.ppermute(value, axis, [(source, (source + steps) % count) for source...  5.88 us
    pallas_call x1, Pallas kernels, dispatch(): pl.pallas_call(dispatch_kernel, out_shape=jax.ShapeDtypeStruct((slots,) +...  3.89 us
  transfers between devices with their start and end apart: 5, of which 4 were waited for; matrix products, arithmetic and copies ran while one was open for 0% of the time, Pallas kernels for 1%

profile of v6, /device:TPU:30, one launch (start us, length us, event | category | flops | bytes accessed | tf_op | source)
XLA Modules:
  0.0 70.3 jit_solution(8424792086439130053)
XLA Ops:
  1.3 3.9 %dispatch.1 = f32[256,16,128]{2,1,0:T(8,128)} custom-call(s32[128]{0:T(128)} %bitcast.19, s32[1]{0:T(128)S(6)} %copy.8.count_ref, s32[128,256]{1,0:T(8,128)} %offset_hbm.1, f32[3,128,256]{2,1,0:T(8,128)} %bitcast.15, f32[3,128,256]{2,1,0:T(8,128)} %bitcast.16, f32[128,256]{1,0:T(8,128)} %weight_hbm.1), custom_call_target="tpu_custom_call" | custom-call | tf_op jit(solution)/shard_map/dispatch/pallas_call | solution.py:82
  5.2 10.2 %all-to-all-start = ((f32[256,16,128]{2,1,0:T(8,128)}), f32[256,16,128]{2,1,0:T(8,128)S(1)}, u32[]{:S(2)}, u32[]{:S(2)}) async-start(f32[256,16,128]{2,1,0:T(8,128)} %dispatch.1), calls=%async_computation | async-start | bytes 4194304 | tf_op jit(solution)/shard_map/all_to_all | solution.py:335
  15.4 27.9 %all-to-all-done = f32[256,16,128]{2,1,0:T(8,128)S(1)} async-done(((f32[256,16,128]{2,1,0:T(8,128)}), f32[256,16,128]{2,1,0:T(8,128)S(1)}, u32[]{:S(2)}, u32[]{:S(2)}) %all-to-all-start) | async-done | bytes 2097184 | tf_op jit(solution)/shard_map/all_to_all | solution.py:335
  43.3 11.5 %splat.1 = (f32[2,4,8,128]{3,2,1,0:T(8,128)S(1)}, f32[24,128]{1,0:T(8,128)S(1)}, f32[24,128]{1,0:T(8,128)S(1)}, f32[8,128]{1,0:T(8,128)S(1)}, f32[8,128]{1,0:T(8,128)S(1)}) custom-call(f32[4096,128]{1,0:T(8,128)S(1)} %bitcast.14), custom_call_target="tpu_custom_call" | custom-call | tf_op jit(solution)/shard_map/splat/pallas_call | solution.py:258
  54.8 0.0 collective-permute-start
  54.9 2.9 %collective-permute-start.1 = (f32[24,128]{1,0:T(8,128)S(1)}, f32[24,128]{1,0:T(8,128)S(1)}, u32[]{:S(2)}, u32[]{:S(2)}) collective-permute-start(f32[24,128]{1,0:T(8,128)S(1)} %get-tuple-element.11), channel_id=1, source_target_pairs={{0,112},{16,0},{32,16},{48,32},{64,48},{80,64},{96,80},{112,96},{1... | collective-permute-start | bytes 36872 | tf_op jit(solution)/shard_map/ppermute | solution.py:28
  57.8 0.1 pad_add_fusion.edge_ref
  57.9 1.3 %collective-permute-done.below_ref = f32[24,128]{1,0:T(8,128)S(1)} collective-permute-done((f32[24,128]{1,0:T(8,128)S(1)}, f32[24,128]{1,0:T(8,128)S(1)}, u32[]{:S(2)}, u32[]{:S(2)}) %collective-permute-start) | collective-permute-done | bytes 12320 | tf_op jit(solution)/shard_map/ppermute | solution.py:28
  59.2 0.0 collective-permute-done.1.above_ref
  59.2 0.6 join.1
  59.8 2.9 %collective-permute-start.2 = (f32[8,128]{1,0:T(8,128)S(1)}, f32[8,128]{1,0:T(8,128)S(1)}, u32[]{:S(2)}, u32[]{:S(2)}) collective-permute-start(f32[8,128]{1,0:T(8,128)S(1)} %get-tuple-element.14), channel_id=1, source_target_pairs={{0,1},{1,2},{2,3},{3,4},{4,5},{5,6},{6,7},{7,8},{8,9},{9,10},{10,1... | collective-permute-start | bytes 12296 | tf_op jit(solution)/shard_map/ppermute | solution.py:28
  62.7 0.0 collective-permute-start.3
  62.7 0.6 widen.1
  63.2 0.8 %collective-permute-done.2 = f32[8,128]{1,0:T(8,128)S(1)} collective-permute-done((f32[8,128]{1,0:T(8,128)S(1)}, f32[8,128]{1,0:T(8,128)S(1)}, u32[]{:S(2)}, u32[]{:S(2)}) %collective-permute-start.2) | collective-permute-done | bytes 4128 | tf_op jit(solution)/shard_map/ppermute | solution.py:28
  64.0 5.6 %collective-permute-done.3 = f32[8,128]{1,0:T(8,128)S(1)} collective-permute-done((f32[8,128]{1,0:T(8,128)S(1)}, f32[8,128]{1,0:T(8,128)S(1)}, u32[]{:S(2)}, u32[]{:S(2)}) %collective-permute-start.3) | collective-permute-done | bytes 4128 | tf_op jit(solution)/shard_map/ppermute | solution.py:28
  69.6 0.1 select_add_fusion
  69.7 0.6 slice_bitcast_fusion
  (1 shorter events, 0.0 us)
Async XLA Ops:
  5.2 38.1 %all-to-all-start = ((f32[256,16,128]{2,1,0:T(8,128)}), f32[256,16,128]{2,1,0:T(8,128)S(1)}, u32[]{:S(2)}, u32[]{:S(2)}) async-start(f32[256,16,128]{2,1,0:T(8,128)} %dispatch.1), calls=%async_computation | async-start | bytes 4194304 | tf_op jit(solution)/shard_map/all_to_all | solution.py:335
  54.8 4.3 %collective-permute-start = (f32[24,128]{1,0:T(8,128)S(1)}, f32[24,128]{1,0:T(8,128)S(1)}, u32[]{:S(2)}, u32[]{:S(2)}) collective-permute-start(f32[24,128]{1,0:T(8,128)S(1)} %get-tuple-element.10), channel_id=1, source_target_pairs={{0,16},{16,32},{32,48},{48,64},{64,80},{80,96},{96,112},{112,0},{1... | collective-permute-start | bytes 36872 | tf_op jit(solution)/shard_map/ppermute | solution.py:28
  54.9 4.3 %collective-permute-start.1 = (f32[24,128]{1,0:T(8,128)S(1)}, f32[24,128]{1,0:T(8,128)S(1)}, u32[]{:S(2)}, u32[]{:S(2)}) collective-permute-start(f32[24,128]{1,0:T(8,128)S(1)} %get-tuple-element.11), channel_id=1, source_target_pairs={{0,112},{16,0},{32,16},{48,32},{64,48},{80,64},{96,80},{112,96},{1... | collective-permute-start | bytes 36872 | tf_op jit(solution)/shard_map/ppermute | solution.py:28
  59.8 4.2 %collective-permute-start.2 = (f32[8,128]{1,0:T(8,128)S(1)}, f32[8,128]{1,0:T(8,128)S(1)}, u32[]{:S(2)}, u32[]{:S(2)}) collective-permute-start(f32[8,128]{1,0:T(8,128)S(1)} %get-tuple-element.14), channel_id=1, source_target_pairs={{0,1},{1,2},{2,3},{3,4},{4,5},{5,6},{6,7},{7,8},{8,9},{9,10},{10,1... | collective-permute-start | bytes 12296 | tf_op jit(solution)/shard_map/ppermute | solution.py:28
  62.7 6.9 %collective-permute-start.3 = (f32[8,128]{1,0:T(8,128)S(1)}, f32[8,128]{1,0:T(8,128)S(1)}, u32[]{:S(2)}, u32[]{:S(2)}) collective-permute-start(f32[8,128]{1,0:T(8,128)S(1)} %get-tuple-element.15), channel_id=1, source_target_pairs={{0,15},{1,0},{2,1},{3,2},{4,3},{5,4},{6,5},{7,6},{8,7},{9,8},{10,9... | collective-permute-start | bytes 12296 | tf_op jit(solution)/shard_map/ppermute | solution.py:28

commit v7 on v6

--- a/solution.py
+++ b/solution.py
@@ -296,15 +296,15 @@
     )(edges, below, above, right, left)
 
 
-def widen_kernel(edge_ref, field_ref, below_ref, above_ref, out_ref):
-    for k in range(2):
+def widen_kernel(edge_ref, field_ref, below_ref, above_ref, rhs_ref, screen_ref):
+    for k, out_ref in enumerate((rhs_ref, screen_ref)):
         for r in range(BX):
             plane = field_ref[k, r]
             if r == 0:
                 plane = plane + jnp.where(edge_ref[0] == 0, 0.0, below_ref[BY * k : BY * k + BY, :])
             if r == BX - 1:
                 plane = plane + jnp.where(edge_ref[1] == 0, 0.0, above_ref[BY * k : BY * k + BY, :])
-            out_ref[k, r] = plane
+            out_ref[r] = plane
 
 
 def widen(edges, field, below, above):
@@ -312,9 +312,9 @@
     vmem = pl.BlockSpec(memory_space=pltpu.VMEM)
     return pl.pallas_call(
         widen_kernel,
-        out_shape=jax.ShapeDtypeStruct(field.shape, jnp.float32),
+        out_shape=(jax.ShapeDtypeStruct(field.shape[1:], jnp.float32),) * 2,
         in_specs=[smem] + [vmem] * 3,
-        out_specs=vmem,
+        out_specs=(vmem, vmem),
         cost_estimate=pl.CostEstimate(flops=20000000, bytes_accessed=100000, transcendentals=0),
         compiler_params=pltpu.CompilerParams(vmem_limit_bytes=4 * 1024 * 1024),
         name="widen",
@@ -341,14 +341,15 @@
     right, left = join(edges, below, above, right, left)
     before = passed_along(right, "yz", 1)
     after = passed_along(left, "yz", -1)
-    field = widen(edges, field, below, above)
-    row = lax.broadcasted_iota(jnp.int32, (1, 1, BY, 1), 2)
+    planes = widen(edges, field, below, above)
+    row = lax.broadcasted_iota(jnp.int32, (1, BY, 1), 1)
     first = (row == 0) & (column > 0)
     last = (row == BY - 1) & (column < columns - 1)
-    before = jnp.where(first, before.reshape(2, BX, 1, BZ), 0.0)
-    after = jnp.where(last, after.reshape(2, BX, 1, BZ), 0.0)
-    total = field + before + after
-    return total[0], total[1]
+    out = []
+    for k, plane in enumerate(planes):
+        part = slice(BX * k, BX * k + BX)
+        out.append(plane + jnp.where(first, before[part, None], 0.0) + jnp.where(last, after[part, None], 0.0))
+    return tuple(out)
 
 
 def solution(mesh):

time: 70.5 us -> 70.5 us (level)
  no operation moved by 1% of the time
where the time goes in v7:
time: 70.5 us; the launch traced here: 70.3 us
  waiting for transfers between devices  35.6 us (50%)
  Pallas kernels  16.5 us (23%)
  starting transfers between devices  16.1 us (23%)
  between operations  1.34 us (2%)
  other arithmetic  0.77 us (1%)
    all_to_all x1, waiting for transfers between devices, shards(): lax.all_to_all(outbox, ('gx', 'yz'), split_axis=0, concat_axis=0, tiled=T...  27.9 us
    pallas_call x1, Pallas kernels, splat(): pl.pallas_call(splat_kernel, out_shape=tuple((jax.ShapeDtypeStruct(shape,...  11.5 us
    all_to_all x1, starting transfers between devices, shards(): lax.all_to_all(outbox, ('gx', 'yz'), split_axis=0, concat_axis=0, tiled=T...  10.2 us
    ppermute x4, waiting for transfers between devices, passed_along(): lax.ppermute(value, axis, [(source, (source + steps) % count) for source...  7.69 us
    ppermute x4, starting transfers between devices, passed_along(): lax.ppermute(value, axis, [(source, (source + steps) % count) for source...  5.88 us
    pallas_call x1, Pallas kernels, dispatch(): pl.pallas_call(dispatch_kernel, out_shape=jax.ShapeDtypeStruct((slots,) +...  3.88 us
  transfers between devices with their start and end apart: 5, of which 4 were waited for; matrix products, arithmetic and copies ran while one was open for 0% of the time, Pallas kernels for 1%

profile of v7, /device:TPU:30, one launch (start us, length us, event | category | flops | bytes accessed | tf_op | source)
XLA Modules:
  0.0 70.3 jit_solution(1887146128432584341)
XLA Ops:
  1.3 3.9 %dispatch.1 = f32[256,16,128]{2,1,0:T(8,128)} custom-call(s32[128]{0:T(128)} %bitcast.11, s32[1]{0:T(128)S(6)} %copy.8.count_ref, s32[128,256]{1,0:T(8,128)} %offset_hbm.1, f32[3,128,256]{2,1,0:T(8,128)} %bitcast.9, f32[3,128,256]{2,1,0:T(8,128)} %bitcast.10, f32[128,256]{1,0:T(8,128)} %weight_hbm.1), custom_call_target="tpu_custom_call" | custom-call | tf_op jit(solution)/shard_map/dispatch/pallas_call | solution.py:82
  5.2 10.2 %all-to-all-start = ((f32[256,16,128]{2,1,0:T(8,128)}), f32[256,16,128]{2,1,0:T(8,128)S(1)}, u32[]{:S(2)}, u32[]{:S(2)}) async-start(f32[256,16,128]{2,1,0:T(8,128)} %dispatch.1), calls=%async_computation | async-start | bytes 4194304 | tf_op jit(solution)/shard_map/all_to_all | solution.py:335
  15.4 27.9 %all-to-all-done = f32[256,16,128]{2,1,0:T(8,128)S(1)} async-done(((f32[256,16,128]{2,1,0:T(8,128)}), f32[256,16,128]{2,1,0:T(8,128)S(1)}, u32[]{:S(2)}, u32[]{:S(2)}) %all-to-all-start) | async-done | bytes 2097184 | tf_op jit(solution)/shard_map/all_to_all | solution.py:335
  43.3 11.5 %splat.1 = (f32[2,4,8,128]{3,2,1,0:T(8,128)S(1)}, f32[24,128]{1,0:T(8,128)S(1)}, f32[24,128]{1,0:T(8,128)S(1)}, f32[8,128]{1,0:T(8,128)S(1)}, f32[8,128]{1,0:T(8,128)S(1)}) custom-call(f32[4096,128]{1,0:T(8,128)S(1)} %bitcast.8), custom_call_target="tpu_custom_call" | custom-call | tf_op jit(solution)/shard_map/splat/pallas_call | solution.py:258
  54.8 0.0 collective-permute-start
  54.8 2.9 %collective-permute-start.1 = (f32[24,128]{1,0:T(8,128)S(1)}, f32[24,128]{1,0:T(8,128)S(1)}, u32[]{:S(2)}, u32[]{:S(2)}) collective-permute-start(f32[24,128]{1,0:T(8,128)S(1)} %get-tuple-element.13), channel_id=1, source_target_pairs={{0,112},{16,0},{32,16},{48,32},{64,48},{80,64},{96,80},{112,96},{1... | collective-permute-start | bytes 36872 | tf_op jit(solution)/shard_map/ppermute | solution.py:28
  57.8 0.1 pad_add_fusion.edge_ref
  57.9 1.3 %collective-permute-done.below_ref = f32[24,128]{1,0:T(8,128)S(1)} collective-permute-done((f32[24,128]{1,0:T(8,128)S(1)}, f32[24,128]{1,0:T(8,128)S(1)}, u32[]{:S(2)}, u32[]{:S(2)}) %collective-permute-start) | collective-permute-done | bytes 12320 | tf_op jit(solution)/shard_map/ppermute | solution.py:28
  59.2 0.0 collective-permute-done.1.above_ref
  59.2 0.6 join.1
  59.8 2.9 %collective-permute-start.2 = (f32[8,128]{1,0:T(8,128)S(1)}, f32[8,128]{1,0:T(8,128)S(1)}, u32[]{:S(2)}, u32[]{:S(2)}) collective-permute-start(f32[8,128]{1,0:T(8,128)S(1)} %get-tuple-element.17), channel_id=1, source_target_pairs={{0,1},{1,2},{2,3},{3,4},{4,5},{5,6},{6,7},{7,8},{8,9},{9,10},{10,1... | collective-permute-start | bytes 12296 | tf_op jit(solution)/shard_map/ppermute | solution.py:28
  62.7 0.0 collective-permute-start.3
  62.7 0.6 widen.1
  63.2 0.8 %collective-permute-done.2 = f32[8,128]{1,0:T(8,128)S(1)} collective-permute-done((f32[8,128]{1,0:T(8,128)S(1)}, f32[8,128]{1,0:T(8,128)S(1)}, u32[]{:S(2)}, u32[]{:S(2)}) %collective-permute-start.2) | collective-permute-done | bytes 4128 | tf_op jit(solution)/shard_map/ppermute | solution.py:28
  64.0 5.6 %collective-permute-done.3 = f32[8,128]{1,0:T(8,128)S(1)} collective-permute-done((f32[8,128]{1,0:T(8,128)S(1)}, f32[8,128]{1,0:T(8,128)S(1)}, u32[]{:S(2)}, u32[]{:S(2)}) %collective-permute-start.3) | collective-permute-done | bytes 4128 | tf_op jit(solution)/shard_map/ppermute | solution.py:28
  69.6 0.7 select_add_fusion
  (3 shorter events, 0.0 us)
Async XLA Ops:
  5.2 38.1 %all-to-all-start = ((f32[256,16,128]{2,1,0:T(8,128)}), f32[256,16,128]{2,1,0:T(8,128)S(1)}, u32[]{:S(2)}, u32[]{:S(2)}) async-start(f32[256,16,128]{2,1,0:T(8,128)} %dispatch.1), calls=%async_computation | async-start | bytes 4194304 | tf_op jit(solution)/shard_map/all_to_all | solution.py:335
  54.8 4.3 %collective-permute-start = (f32[24,128]{1,0:T(8,128)S(1)}, f32[24,128]{1,0:T(8,128)S(1)}, u32[]{:S(2)}, u32[]{:S(2)}) collective-permute-start(f32[24,128]{1,0:T(8,128)S(1)} %get-tuple-element.12), channel_id=1, source_target_pairs={{0,16},{16,32},{32,48},{48,64},{64,80},{80,96},{96,112},{112,0},{1... | collective-permute-start | bytes 36872 | tf_op jit(solution)/shard_map/ppermute | solution.py:28
  54.8 4.3 %collective-permute-start.1 = (f32[24,128]{1,0:T(8,128)S(1)}, f32[24,128]{1,0:T(8,128)S(1)}, u32[]{:S(2)}, u32[]{:S(2)}) collective-permute-start(f32[24,128]{1,0:T(8,128)S(1)} %get-tuple-element.13), channel_id=1, source_target_pairs={{0,112},{16,0},{32,16},{48,32},{64,48},{80,64},{96,80},{112,96},{1... | collective-permute-start | bytes 36872 | tf_op jit(solution)/shard_map/ppermute | solution.py:28
  59.8 4.2 %collective-permute-start.2 = (f32[8,128]{1,0:T(8,128)S(1)}, f32[8,128]{1,0:T(8,128)S(1)}, u32[]{:S(2)}, u32[]{:S(2)}) collective-permute-start(f32[8,128]{1,0:T(8,128)S(1)} %get-tuple-element.17), channel_id=1, source_target_pairs={{0,1},{1,2},{2,3},{3,4},{4,5},{5,6},{6,7},{7,8},{8,9},{9,10},{10,1... | collective-permute-start | bytes 12296 | tf_op jit(solution)/shard_map/ppermute | solution.py:28
  62.7 6.9 %collective-permute-start.3 = (f32[8,128]{1,0:T(8,128)S(1)}, f32[8,128]{1,0:T(8,128)S(1)}, u32[]{:S(2)}, u32[]{:S(2)}) collective-permute-start(f32[8,128]{1,0:T(8,128)S(1)} %get-tuple-element.18), channel_id=1, source_target_pairs={{0,15},{1,0},{2,1},{3,2},{4,3},{5,4},{6,5},{7,6},{8,7},{9,8},{10,9... | collective-permute-start | bytes 12296 | tf_op jit(solution)/shard_map/ppermute | solution.py:28
